TPU v7x, 128 devices: a whole 4x4x4 slice. The times are simulated.
128 devices in a mesh: dp: 1, tp: 2 (over core), cp: 64 (over z, y, x).
Axes of the slice: x: 4, y: 4, z: 4, core: 2. Of those that a mesh axis runs over, the one named last changes fastest.
Arguments:
- tokens: bfloat16 [12288, 3072], P(('dp', 'tp', 'cp'))
- norm_attn: bfloat16 [2, 3072], replicated
- norm_mlp: bfloat16 [2, 3072], replicated
- w_q: bfloat16 [2, 3072, 24, 128], P(None, None, 'tp')
- w_k: bfloat16 [2, 3072, 1024], P(None, None, 'tp')
- w_v: bfloat16 [2, 3072, 1024], P(None, None, 'tp')
- w_o: bfloat16 [2, 24, 128, 3072], P(None, 'tp')
- w_gate: bfloat16 [2, 3072, 8192], P(None, None, 'tp')
- w_up: bfloat16 [2, 3072, 8192], P(None, None, 'tp')
- w_down: bfloat16 [2, 8192, 3072], P(None, 'tp')
Outputs:
- output: bfloat16 [12288, 3072], P(('dp', 'tp', 'cp'))
All inputs are finite; a program needn't handle non-finite values.
Results may differ from a plain program's by a relative error of at most 0.02.
Values are sent between devices in bfloat16 or wider.
A program may use at most 1 GiB of HBM per device.

v0:
```python
import math
import jax
import jax.numpy as jnp
from jax import lax
from jax.sharding import PartitionSpec as P, NamedSharding


def rms_norm(hidden, gain):
    hidden_f = hidden.astype(jnp.float32)
    inv_rms = lax.rsqrt(jnp.mean(hidden_f * hidden_f, axis=-1, keepdims=True) + 1e-5)
    return (hidden_f * inv_rms * gain.astype(jnp.float32)).astype(jnp.bfloat16)


def rotary(values, positions):
    half_dim = values.shape[-1] // 2
    inv_freq = 500000.0 ** (-(jnp.arange(half_dim, dtype=jnp.float32) * 2.0 / values.shape[-1]))
    angles = positions.astype(jnp.float32)[:, None] * inv_freq[None, :]
    cos_ang = jnp.cos(angles)[:, None, :]
    sin_ang = jnp.sin(angles)[:, None, :]
    first = values[..., :half_dim]
    second = values[..., half_dim:]
    return jnp.concatenate([first * cos_ang - second * sin_ang, second * cos_ang + first * sin_ang], axis=-1)


def seg_positions(dev_ids, rows, dev_total):
    offset = jnp.arange(rows)
    half_len = rows // 2
    seg_idx = jnp.where(offset < half_len, dev_ids[..., None], 2 * dev_total - 1 - dev_ids[..., None])
    return seg_idx * half_len + offset % half_len


def attend(queries, keys_all, values_all, q_pos, k_pos, block_rows):
    rows, kv_loc, group, head_dim = queries.shape
    scale = 1.0 / math.sqrt(head_dim)
    q_blocks = queries.reshape(rows // block_rows, block_rows, kv_loc, group, head_dim)
    pos_blocks = q_pos.reshape(rows // block_rows, block_rows)

    def one_block(block):
        q_blk, pos_blk = block
        scores = jnp.einsum('bkgd,tkd->bkgt', q_blk, keys_all, preferred_element_type=jnp.float32) * scale
        visible = k_pos[None, None, None, :] <= pos_blk[:, None, None, None]
        scores = jnp.where(visible, scores, -jnp.inf)
        weights = jnp.exp(scores - jnp.max(scores, axis=-1, keepdims=True))
        row_sum = jnp.sum(weights, axis=-1, keepdims=True)
        mixed = jnp.einsum('bkgt,tkd->bkgd', weights.astype(jnp.bfloat16), values_all, preferred_element_type=jnp.float32)
        return (mixed / row_sum).astype(jnp.bfloat16)

    return lax.map(one_block, (q_blocks, pos_blocks)).reshape(rows, kv_loc * group, head_dim)


def solution(mesh):
    tp_size = mesh.shape['tp']
    cp_size = mesh.shape['cp']
    dev_total = tp_size * cp_size
    row_spec = P(('dp', 'tp', 'cp'), None)
    gain_spec = P(None, None)
    q_spec = P(None, None, 'tp', None)
    col_spec = P(None, None, 'tp')
    o_spec = P(None, 'tp', None, None)
    down_spec = P(None, 'tp', None)

    def body(tokens, norm_attn, norm_mlp, w_q, w_k, w_v, w_o, w_gate, w_up, w_down):
        rows = tokens.shape[0]
        heads_loc = w_q.shape[2]
        head_dim = w_q.shape[3]
        kv_cols = w_k.shape[2]
        tp_idx = lax.axis_index('tp')
        cp_idx = lax.axis_index('cp')
        tp_devs = jnp.arange(tp_size) * cp_size + cp_idx
        pos_rows = seg_positions(tp_devs, rows, dev_total).reshape(tp_size * rows)
        key_devs = jnp.arange(cp_size)[:, None] + jnp.arange(tp_size)[None, :] * cp_size
        pos_keys = seg_positions(key_devs, rows, dev_total).reshape(dev_total * rows)
        hidden = tokens
        for layer_idx in range(w_q.shape[0]):
            normed = lax.all_gather(rms_norm(hidden, norm_attn[layer_idx]), 'tp', axis=0, tiled=True)
            q_proj = jnp.einsum('rd,dhe->rhe', normed, w_q[layer_idx], preferred_element_type=jnp.float32)
            queries = rotary(q_proj, pos_rows).astype(jnp.bfloat16)
            wk_loc = w_k[layer_idx]
            wv_loc = w_v[layer_idx]
            if kv_cols >= head_dim:
                kv_loc = kv_cols // head_dim
            else:
                kv_total = kv_cols * tp_size // head_dim
                start = (tp_idx * kv_total // tp_size) * head_dim
                wk_loc = lax.dynamic_slice_in_dim(lax.all_gather(wk_loc, 'tp', axis=1, tiled=True), start, head_dim, axis=1)
                wv_loc = lax.dynamic_slice_in_dim(lax.all_gather(wv_loc, 'tp', axis=1, tiled=True), start, head_dim, axis=1)
                kv_loc = 1
            k_proj = jnp.dot(normed, wk_loc, preferred_element_type=jnp.float32)
            keys_loc = rotary(k_proj.reshape(tp_size * rows, kv_loc, head_dim), pos_rows).astype(jnp.bfloat16)
            values_loc = jnp.dot(normed, wv_loc, preferred_element_type=jnp.float32).astype(jnp.bfloat16).reshape(tp_size * rows, kv_loc, head_dim)
            keys_all = lax.all_gather(keys_loc, 'cp', axis=0, tiled=True)
            values_all = lax.all_gather(values_loc, 'cp', axis=0, tiled=True)
            grouped = queries.reshape(tp_size * rows, kv_loc, heads_loc // kv_loc, head_dim)
            mixed = attend(grouped, keys_all, values_all, pos_rows, pos_keys, rows // 2)
            attn_part = jnp.einsum('rhe,hed->rd', mixed, w_o[layer_idx], preferred_element_type=jnp.float32)
            attn_out = lax.psum_scatter(attn_part, 'tp', scatter_dimension=0, tiled=True)
            hidden_mid = (hidden.astype(jnp.float32) + attn_out).astype(jnp.bfloat16)
            normed_mlp = lax.all_gather(rms_norm(hidden_mid, norm_mlp[layer_idx]), 'tp', axis=0, tiled=True)
            gate_pre = jnp.dot(normed_mlp, w_gate[layer_idx], preferred_element_type=jnp.float32)
            up_proj = jnp.dot(normed_mlp, w_up[layer_idx], preferred_element_type=jnp.float32)
            hidden_act = (jax.nn.silu(gate_pre) * up_proj).astype(jnp.bfloat16)
            mlp_part = jnp.dot(hidden_act, w_down[layer_idx], preferred_element_type=jnp.float32)
            mlp_out = lax.psum_scatter(mlp_part, 'tp', scatter_dimension=0, tiled=True)
            hidden = (hidden_mid.astype(jnp.float32) + mlp_out).astype(jnp.bfloat16)
        return hidden

    return jax.shard_map(
        body,
        mesh=mesh,
        in_specs=(row_spec, gain_spec, gain_spec, q_spec, col_spec, col_spec, o_spec, col_spec, col_spec, down_spec),
        out_specs=row_spec,
        check_vma=False,
    )
```

profile of v0, /device:TPU:1, one launch (start us, length us, event | category | flops | bytes accessed | tf_op | source)
XLA Modules:
  0.0 966.9 jit_solution(925344123961467414)
XLA Ops:
  41.9 80.0 %all-gather.11.cloned.1.call-done = bf16[12288,4,128]{2,0,1:T(8,128)(2,1)} async-done(((bf16[192,4,128]{2,0,1:T(8,128)(2,1)}), bf16[12288,4,128]{2,0,1:T(8,128)(2,1)}) %all-gather.11.cloned.1.call-update) | async-done | bytes 12582928 | tf_op jit(solution)/shard_map/all_gather | solution.py:91
  122.0 93.1 %all-gather.13.cloned.1.call-done = bf16[12288,4,128]{2,0,1:T(8,128)(2,1)} async-done(((bf16[192,4,128]{2,0,1:T(8,128)(2,1)}), bf16[12288,4,128]{2,0,1:T(8,128)(2,1)}) %all-gather.13.cloned.1.call-update) | async-done | bytes 12582928 | tf_op jit(solution)/shard_map/all_gather | solution.py:92
  215.2 184.8 %while.22 = (s32[]{:T(128)}, bf16[4,48,4,3,128]{4,1,0,3,2:T(8,128)(2,1)S(1)}, s32[4,48]{1,0:T(4,128)S(1)}, bf16[4,48,4,3,128]{4,1,0,3,2:T(8,128)(2,1)S(1)}, bf16...) while((s32[]{:T(128)}, ...), condition=%wide.region_4.5_spmd.clone, body=%wide.region_1.4_spmd.clone.sunk | while | flops 3702508544 | bytes 112976784 | solution.py:48
  243.2 18.1 %fusion.224 = bf16[4,48,4,3,128]{4,1,0,3,2:T(8,128)(2,1)S(1)} fusion(bf16[4,48,4,3,128]{4,1,0,3,2:T(8,128)(2,1)S(1)} %get-tuple-element.345, s32[]{:T(128)} %get-tuple-element.344, bf16[12288,4,128]{2,0,1:T(8,128)(2,1)} %get-tuple-element.360, f32[4,48,3,12288]{3,1,2,0:T(8,128)} %get-tuple-element.319, f32[48,4,3]{0,2,1:T(4,128)S(1)} %get-tuple-element.320, ...), kind=kOutput, calls=%fused_computation.21.clone.1 | convolution fusion | flops 1840398336 | bytes 41648132 | tf_op jit(solution)/shard_map/while/body/eval_jaxpr/bkgt,tkd->bkgd/dot_general | solution.py:45
  262.1 14.3 %bitcast_reduce_fusion.4 = (f32[48,4,3]{0,2,1:T(4,128)S(1)}, f32[4,48,3,12288]{3,1,2,0:T(8,128)}) fusion(pred[48,12288]{1,0:T(8,128)(4,1)S(1)} %broadcast_compare_fusion.4, bf16[12288,4,128]{2,0,1:T(8,128)(2,1)} %get-tuple-element.359, bf16[4,48,4,3,128]{4,1,0,3,2:T(8,128)(2,1)S(1)} %get-tuple-element.358, s32[]{:T(128)} %get-tuple-element.344), kind=kOutput, calls=%fused_computation.3.clone.1 | convolution fusion | flops 1833172480 | bytes 41634052 | tf_op jit(solution)/shard_map/while/body/eval_jaxpr/bkgd,tkd->bkgt/dot_general | solution.py:40
  289.5 18.1 %fusion.224 = bf16[4,48,4,3,128]{4,1,0,3,2:T(8,128)(2,1)S(1)} fusion(bf16[4,48,4,3,128]{4,1,0,3,2:T(8,128)(2,1)S(1)} %get-tuple-element.345, s32[]{:T(128)} %get-tuple-element.344, bf16[12288,4,128]{2,0,1:T(8,128)(2,1)} %get-tuple-element.360, f32[4,48,3,12288]{3,1,2,0:T(8,128)} %get-tuple-element.319, f32[48,4,3]{0,2,1:T(4,128)S(1)} %get-tuple-element.320, ...), kind=kOutput, calls=%fused_computation.21.clone.1 | convolution fusion | flops 1840398336 | bytes 41648132 | tf_op jit(solution)/shard_map/while/body/eval_jaxpr/bkgt,tkd->bkgd/dot_general | solution.py:45
  308.3 14.3 %bitcast_reduce_fusion.4 = (f32[48,4,3]{0,2,1:T(4,128)S(1)}, f32[4,48,3,12288]{3,1,2,0:T(8,128)}) fusion(pred[48,12288]{1,0:T(8,128)(4,1)S(1)} %broadcast_compare_fusion.4, bf16[12288,4,128]{2,0,1:T(8,128)(2,1)} %get-tuple-element.359, bf16[4,48,4,3,128]{4,1,0,3,2:T(8,128)(2,1)S(1)} %get-tuple-element.358, s32[]{:T(128)} %get-tuple-element.344), kind=kOutput, calls=%fused_computation.3.clone.1 | convolution fusion | flops 1833172480 | bytes 41634052 | tf_op jit(solution)/shard_map/while/body/eval_jaxpr/bkgd,tkd->bkgt/dot_general | solution.py:40
  335.7 18.1 %fusion.224 = bf16[4,48,4,3,128]{4,1,0,3,2:T(8,128)(2,1)S(1)} fusion(bf16[4,48,4,3,128]{4,1,0,3,2:T(8,128)(2,1)S(1)} %get-tuple-element.345, s32[]{:T(128)} %get-tuple-element.344, bf16[12288,4,128]{2,0,1:T(8,128)(2,1)} %get-tuple-element.360, f32[4,48,3,12288]{3,1,2,0:T(8,128)} %get-tuple-element.319, f32[48,4,3]{0,2,1:T(4,128)S(1)} %get-tuple-element.320, ...), kind=kOutput, calls=%fused_computation.21.clone.1 | convolution fusion | flops 1840398336 | bytes 41648132 | tf_op jit(solution)/shard_map/while/body/eval_jaxpr/bkgt,tkd->bkgd/dot_general | solution.py:45
  354.5 14.3 %bitcast_reduce_fusion.4 = (f32[48,4,3]{0,2,1:T(4,128)S(1)}, f32[4,48,3,12288]{3,1,2,0:T(8,128)}) fusion(pred[48,12288]{1,0:T(8,128)(4,1)S(1)} %broadcast_compare_fusion.4, bf16[12288,4,128]{2,0,1:T(8,128)(2,1)} %get-tuple-element.359, bf16[4,48,4,3,128]{4,1,0,3,2:T(8,128)(2,1)S(1)} %get-tuple-element.358, s32[]{:T(128)} %get-tuple-element.344), kind=kOutput, calls=%fused_computation.3.clone.1 | convolution fusion | flops 1833172480 | bytes 41634052 | tf_op jit(solution)/shard_map/while/body/eval_jaxpr/bkgd,tkd->bkgt/dot_general | solution.py:40
  381.9 18.1 %fusion.224 = bf16[4,48,4,3,128]{4,1,0,3,2:T(8,128)(2,1)S(1)} fusion(bf16[4,48,4,3,128]{4,1,0,3,2:T(8,128)(2,1)S(1)} %get-tuple-element.345, s32[]{:T(128)} %get-tuple-element.344, bf16[12288,4,128]{2,0,1:T(8,128)(2,1)} %get-tuple-element.360, f32[4,48,3,12288]{3,1,2,0:T(8,128)} %get-tuple-element.319, f32[48,4,3]{0,2,1:T(4,128)S(1)} %get-tuple-element.320, ...), kind=kOutput, calls=%fused_computation.21.clone.1 | convolution fusion | flops 1840398336 | bytes 41648132 | tf_op jit(solution)/shard_map/while/body/eval_jaxpr/bkgt,tkd->bkgd/dot_general | solution.py:45
  434.9 14.6 %fusion.100 = f32[192,4096]{1,0:T(8,128)} fusion(bf16[192,3072]{1,0:T(8,128)(2,1)} %all-gather.15.cloned.1.call-done, bf16[2,3072,4096]{2,1,0:T(8,128)(2,1)} %param.21), kind=kOutput, calls=%fused_computation.68 | convolution fusion | flops 4831838208 | bytes 29491200 | tf_op jit(solution)/shard_map/dot_general | solution.py:99
  449.6 20.7 %fusion.96 = f32[192,3072]{1,0:T(8,128)} fusion(bf16[2,4096,3072]{2,1,0:T(8,128)(2,1)} %param.23, bf16[192,3072]{1,0:T(8,128)(2,1)S(1)} %copy-done.12, bf16[2,3072,4096]{2,1,0:T(8,128)(2,1)} %param.22, f32[192,4096]{1,0:T(8,128)} %fusion.100), kind=kOutput, calls=%fused_computation.64 | convolution fusion | flops 9668395008 | bytes 57016320 | tf_op jit(solution)/shard_map/dot_general | solution.py:102
  514.9 80.8 %all-gather.19.cloned.1.call-done = bf16[12288,4,128]{2,0,1:T(8,128)(2,1)} async-done(((bf16[192,4,128]{2,0,1:T(8,128)(2,1)}), bf16[12288,4,128]{2,0,1:T(8,128)(2,1)}) %all-gather.19.cloned.1.call-update) | async-done | bytes 12582928 | tf_op jit(solution)/shard_map/all_gather | solution.py:91
  595.7 93.1 %all-gather.21.cloned.1.call-done = bf16[12288,4,128]{2,0,1:T(8,128)(2,1)} async-done(((bf16[192,4,128]{2,0,1:T(8,128)(2,1)}), bf16[12288,4,128]{2,0,1:T(8,128)(2,1)}) %all-gather.21.cloned.1.call-update) | async-done | bytes 12582928 | tf_op jit(solution)/shard_map/all_gather | solution.py:92
  688.9 184.8 %while.23 = (s32[]{:T(128)}, bf16[4,48,4,3,128]{4,1,0,3,2:T(8,128)(2,1)S(1)}, s32[4,48]{1,0:T(4,128)S(1)}, bf16[4,48,4,3,128]{4,1,0,3,2:T(8,128)(2,1)S(1)}, bf16...) while((s32[]{:T(128)}, ...), condition=%wide.region_12.13_spmd.clone, body=%wide.region_9.12_spmd.clone.sunk | while | flops 3702508544 | bytes 112976784 | solution.py:48
  716.9 18.1 %fusion.229 = bf16[4,48,4,3,128]{4,1,0,3,2:T(8,128)(2,1)S(1)} fusion(bf16[4,48,4,3,128]{4,1,0,3,2:T(8,128)(2,1)S(1)} %get-tuple-element.378, s32[]{:T(128)} %get-tuple-element.377, bf16[12288,4,128]{2,0,1:T(8,128)(2,1)} %get-tuple-element.393, f32[4,48,3,12288]{3,1,2,0:T(8,128)} %get-tuple-element.331, f32[48,4,3]{0,2,1:T(4,128)S(1)} %get-tuple-element.332, ...), kind=kOutput, calls=%fused_computation.49.clone.1 | convolution fusion | flops 1840398336 | bytes 41648132 | tf_op jit(solution)/shard_map/while/body/eval_jaxpr/bkgt,tkd->bkgd/dot_general | solution.py:45
  735.8 14.3 %bitcast_reduce_fusion.5 = (f32[48,4,3]{0,2,1:T(4,128)S(1)}, f32[4,48,3,12288]{3,1,2,0:T(8,128)}) fusion(pred[48,12288]{1,0:T(8,128)(4,1)S(1)} %broadcast_compare_fusion.5, bf16[12288,4,128]{2,0,1:T(8,128)(2,1)} %get-tuple-element.392, bf16[4,48,4,3,128]{4,1,0,3,2:T(8,128)(2,1)S(1)} %get-tuple-element.391, s32[]{:T(128)} %get-tuple-element.377), kind=kOutput, calls=%fused_computation.31.clone.1 | convolution fusion | flops 1833172480 | bytes 41634052 | tf_op jit(solution)/shard_map/while/body/eval_jaxpr/bkgd,tkd->bkgt/dot_general | solution.py:40
  763.2 18.1 %fusion.229 = bf16[4,48,4,3,128]{4,1,0,3,2:T(8,128)(2,1)S(1)} fusion(bf16[4,48,4,3,128]{4,1,0,3,2:T(8,128)(2,1)S(1)} %get-tuple-element.378, s32[]{:T(128)} %get-tuple-element.377, bf16[12288,4,128]{2,0,1:T(8,128)(2,1)} %get-tuple-element.393, f32[4,48,3,12288]{3,1,2,0:T(8,128)} %get-tuple-element.331, f32[48,4,3]{0,2,1:T(4,128)S(1)} %get-tuple-element.332, ...), kind=kOutput, calls=%fused_computation.49.clone.1 | convolution fusion | flops 1840398336 | bytes 41648132 | tf_op jit(solution)/shard_map/while/body/eval_jaxpr/bkgt,tkd->bkgd/dot_general | solution.py:45
  782.0 14.3 %bitcast_reduce_fusion.5 = (f32[48,4,3]{0,2,1:T(4,128)S(1)}, f32[4,48,3,12288]{3,1,2,0:T(8,128)}) fusion(pred[48,12288]{1,0:T(8,128)(4,1)S(1)} %broadcast_compare_fusion.5, bf16[12288,4,128]{2,0,1:T(8,128)(2,1)} %get-tuple-element.392, bf16[4,48,4,3,128]{4,1,0,3,2:T(8,128)(2,1)S(1)} %get-tuple-element.391, s32[]{:T(128)} %get-tuple-element.377), kind=kOutput, calls=%fused_computation.31.clone.1 | convolution fusion | flops 1833172480 | bytes 41634052 | tf_op jit(solution)/shard_map/while/body/eval_jaxpr/bkgd,tkd->bkgt/dot_general | solution.py:40
  809.4 18.1 %fusion.229 = bf16[4,48,4,3,128]{4,1,0,3,2:T(8,128)(2,1)S(1)} fusion(bf16[4,48,4,3,128]{4,1,0,3,2:T(8,128)(2,1)S(1)} %get-tuple-element.378, s32[]{:T(128)} %get-tuple-element.377, bf16[12288,4,128]{2,0,1:T(8,128)(2,1)} %get-tuple-element.393, f32[4,48,3,12288]{3,1,2,0:T(8,128)} %get-tuple-element.331, f32[48,4,3]{0,2,1:T(4,128)S(1)} %get-tuple-element.332, ...), kind=kOutput, calls=%fused_computation.49.clone.1 | convolution fusion | flops 1840398336 | bytes 41648132 | tf_op jit(solution)/shard_map/while/body/eval_jaxpr/bkgt,tkd->bkgd/dot_general | solution.py:45
  828.2 14.3 %bitcast_reduce_fusion.5 = (f32[48,4,3]{0,2,1:T(4,128)S(1)}, f32[4,48,3,12288]{3,1,2,0:T(8,128)}) fusion(pred[48,12288]{1,0:T(8,128)(4,1)S(1)} %broadcast_compare_fusion.5, bf16[12288,4,128]{2,0,1:T(8,128)(2,1)} %get-tuple-element.392, bf16[4,48,4,3,128]{4,1,0,3,2:T(8,128)(2,1)S(1)} %get-tuple-element.391, s32[]{:T(128)} %get-tuple-element.377), kind=kOutput, calls=%fused_computation.31.clone.1 | convolution fusion | flops 1833172480 | bytes 41634052 | tf_op jit(solution)/shard_map/while/body/eval_jaxpr/bkgd,tkd->bkgt/dot_general | solution.py:40
  855.6 18.1 %fusion.229 = bf16[4,48,4,3,128]{4,1,0,3,2:T(8,128)(2,1)S(1)} fusion(bf16[4,48,4,3,128]{4,1,0,3,2:T(8,128)(2,1)S(1)} %get-tuple-element.378, s32[]{:T(128)} %get-tuple-element.377, bf16[12288,4,128]{2,0,1:T(8,128)(2,1)} %get-tuple-element.393, f32[4,48,3,12288]{3,1,2,0:T(8,128)} %get-tuple-element.331, f32[48,4,3]{0,2,1:T(4,128)S(1)} %get-tuple-element.332, ...), kind=kOutput, calls=%fused_computation.49.clone.1 | convolution fusion | flops 1840398336 | bytes 41648132 | tf_op jit(solution)/shard_map/while/body/eval_jaxpr/bkgt,tkd->bkgd/dot_general | solution.py:45
  908.6 14.6 %fusion.94 = f32[192,4096]{1,0:T(8,128)} fusion(bf16[192,3072]{1,0:T(8,128)(2,1)} %all-gather.23.cloned.1.call-done, bf16[2,3072,4096]{2,1,0:T(8,128)(2,1)} %param.21), kind=kOutput, calls=%fused_computation.62 | convolution fusion | flops 4831838208 | bytes 29491200 | tf_op jit(solution)/shard_map/dot_general | solution.py:99
  923.2 20.7 %fusion.90 = f32[192,3072]{1,0:T(8,128)} fusion(bf16[2,4096,3072]{2,1,0:T(8,128)(2,1)} %param.23, bf16[192,3072]{1,0:T(8,128)(2,1)S(1)} %copy-done.13, bf16[2,3072,4096]{2,1,0:T(8,128)(2,1)} %param.22, f32[192,4096]{1,0:T(8,128)} %fusion.94), kind=kOutput, calls=%fused_computation.58 | convolution fusion | flops 9668395008 | bytes 57016320 | tf_op jit(solution)/shard_map/dot_general | solution.py:102
  (159 shorter events, 304.2 us)
Async XLA Ops:
  6.5 20.4 %all-gather.9.cloned.1.call-start = ((), (), s32[]{:S(2)}) async-start(), calls=%async_computation.4 | async-start | bytes 1769472 | tf_op jit(solution)/shard_map/all_gather | solution.py:75
  11.4 110.6 %all-gather.11.cloned.1.call-start = ((), (), s32[]{:S(2)}) async-start(), calls=%async_computation.5 | async-start | bytes 12779520 | tf_op jit(solution)/shard_map/all_gather | solution.py:91
  21.1 20.0 %copy-start.3 = (f32[192,64]{1,0:T(8,128)}, f32[192,64]{1,0:T(8,128)S(1)}, u32[]{:S(2)}) copy-start(f32[192,64]{1,0:T(8,128)S(1)} %get-tuple-element.197) | copy-start | bytes 147460
  21.1 20.0 %copy-start.5 = (f32[192,64]{1,0:T(8,128)}, f32[192,64]{1,0:T(8,128)S(1)}, u32[]{:S(2)}) copy-start(f32[192,64]{1,0:T(8,128)S(1)} %get-tuple-element.198) | copy-start | bytes 147460
  30.5 4.9 copy-start.7
  30.5 184.6 %all-gather.13.cloned.1.call-start = ((), (), s32[]{:S(2)}) async-start(), calls=%async_computation.6 | async-start | bytes 12779520 | tf_op jit(solution)/shard_map/all_gather | solution.py:92
  34.4 384.7 %reduce-scatter.5.cloned.1.call-start = ((), (), s32[]{:S(2)}) async-start(), calls=%async_computation.7 | async-start | bytes 3538944 | tf_op jit(solution)/shard_map/reduce_scatter | solution.py:96
  400.0 6.5 copy-start.11
  400.0 19.0 %copy-start.2 = (bf16[96,3072]{1,0:T(8,128)(2,1)S(1)}, bf16[96,3072]{1,0:T(8,128)(2,1)}, u32[]{:S(2)}) copy-start(bf16[96,3072]{1,0:T(8,128)(2,1)} %param.14) | copy-start | bytes 1769476
  406.4 28.5 %all-gather.15.cloned.1.call-start = ((), (), s32[]{:S(2)}) async-start(), calls=%async_computation.8 | async-start | bytes 1769472 | tf_op jit(solution)/shard_map/all_gather | solution.py:98
  421.6 62.3 %reduce-scatter.7.cloned.1.call-start = ((), (), s32[]{:S(2)}) async-start(), calls=%async_computation.9 | async-start | bytes 3538944 | tf_op jit(solution)/shard_map/reduce_scatter | solution.py:103
  434.9 14.6 %copy-start.12 = (bf16[192,3072]{1,0:T(8,128)(2,1)S(1)}, bf16[192,3072]{1,0:T(8,128)(2,1)}, u32[]{:S(2)}) copy-start(bf16[192,3072]{1,0:T(8,128)(2,1)} %all-gather.15.cloned.1.call-done) | copy-start | bytes 3538948
  470.2 16.1 %copy-start.9 = (f32[1,3072]{1,0:T(1,128)S(1)}, f32[1,3072]{1,0:T(1,128)}, u32[]{:S(2)}) copy-start(f32[1,3072]{1,0:T(1,128)} %get-tuple-element.195) | copy-start | bytes 36868
  470.2 30.4 %all-gather.17.cloned.1.call-start = ((), (), s32[]{:S(2)}) async-start(), calls=%async_computation.10 | async-start | bytes 1769472 | tf_op jit(solution)/shard_map/all_gather | solution.py:75
  487.4 108.3 %all-gather.19.cloned.1.call-start = ((), (), s32[]{:S(2)}) async-start(), calls=%async_computation.11 | async-start | bytes 12779520 | tf_op jit(solution)/shard_map/all_gather | solution.py:91
  490.6 12.5 %copy-start.4 = (f32[192,64]{1,0:T(8,128)S(1)}, f32[192,64]{1,0:T(8,128)}, u32[]{:S(2)}) copy-start(f32[192,64]{1,0:T(8,128)} %copy-done.3) | copy-start | bytes 147460
  490.6 12.5 %copy-start.6 = (f32[192,64]{1,0:T(8,128)S(1)}, f32[192,64]{1,0:T(8,128)}, u32[]{:S(2)}) copy-start(f32[192,64]{1,0:T(8,128)} %copy-done.5) | copy-start | bytes 147460
  504.2 184.6 %all-gather.21.cloned.1.call-start = ((), (), s32[]{:S(2)}) async-start(), calls=%async_computation.12 | async-start | bytes 12779520 | tf_op jit(solution)/shard_map/all_gather | solution.py:92
  508.1 384.7 %reduce-scatter.9.cloned.1.call-start = ((), (), s32[]{:S(2)}) async-start(), calls=%async_computation.13 | async-start | bytes 3538944 | tf_op jit(solution)/shard_map/reduce_scatter | solution.py:96
  873.7 19.0 %copy-start.1 = (bf16[96,3072]{1,0:T(8,128)(2,1)S(1)}, bf16[96,3072]{1,0:T(8,128)(2,1)}, u32[]{:S(2)}) copy-start(bf16[96,3072]{1,0:T(8,128)(2,1)} %copy-done) | copy-start | bytes 1769476
  880.1 14.2 %copy-start.10 = (f32[1,3072]{1,0:T(1,128)S(1)}, f32[1,3072]{1,0:T(1,128)}, u32[]{:S(2)}) copy-start(f32[1,3072]{1,0:T(1,128)} %get-tuple-element.193) | copy-start | bytes 36868
  880.1 28.5 %all-gather.23.cloned.1.call-start = ((), (), s32[]{:S(2)}) async-start(), calls=%async_computation.14 | async-start | bytes 1769472 | tf_op jit(solution)/shard_map/all_gather | solution.py:98
  895.4 62.2 %reduce-scatter.11.cloned.1.call-start = ((), (), s32[]{:S(2)}) async-start(), calls=%async_computation.15 | async-start | bytes 3538944 | tf_op jit(solution)/shard_map/reduce_scatter | solution.py:103
  908.6 14.6 %copy-start.13 = (bf16[192,3072]{1,0:T(8,128)(2,1)S(1)}, bf16[192,3072]{1,0:T(8,128)(2,1)}, u32[]{:S(2)}) copy-start(bf16[192,3072]{1,0:T(8,128)(2,1)} %all-gather.23.cloned.1.call-done) | copy-start | bytes 3538948
  (2 other events, 5.0 us)
Sparse Core Ops, SparseCore 0:
  11.5 15.4 all-gather.8
  30.6 91.3 all-gather.10
  124.8 90.2 all-gather.12
  406.5 12.4 reduce-scatter.4
  421.8 13.0 all-gather.14
  470.4 13.5 reduce-scatter.6
  487.5 13.0 all-gather.16
  504.3 91.3 all-gather.18
  598.5 90.2 all-gather.20
  880.2 12.4 reduce-scatter.8
  895.5 13.0 all-gather.22
  944.0 13.5 reduce-scatter.10
where the time goes:
time: 972 us; the launch traced here: 967 us
  waiting for transfers between devices  441 us (45%)
  matrix products  365 us (38%)
  other arithmetic  129 us (13%)
  local copies, waits for them, and re-layouts  16.2 us (2%)
  between operations  14.2 us (1%)
    all_gather x2, waiting for transfers between devices, body(): values_all = lax.all_gather(values_loc, 'cp', axis=0, tiled=True)  186 us
    all_gather x2, waiting for transfers between devices, body(): keys_all = lax.all_gather(keys_loc, 'cp', axis=0, tiled=True)  161 us
    dot_general x8, matrix products, one_block(): jnp.einsum('bkgt,tkd->bkgd', weights.astype(jnp.bfloat16), values_all, pr...  145 us
    dot_general x8, matrix products, one_block(): jnp.einsum('bkgd,tkd->bkgt', q_blk, keys_all, preferred_element_type=jnp....  114 us
    reduce_sum x8, other arithmetic, one_block(): row_sum = jnp.sum(weights, axis=-1, keepdims=True)  105 us
    dot_general x2, matrix products, body(): jnp.dot(hidden_act, w_down[layer_idx], preferred_element_type=jnp.float32)  41.3 us
    dot_general x2, matrix products, body(): jnp.dot(normed_mlp, w_gate[layer_idx], preferred_element_type=jnp.float32)  29.2 us
    reduce_scatter x2, waiting for transfers between devices, body(): mlp_out = lax.psum_scatter(mlp_part, 'tp', scatter_dimension=0, tiled=True)  27.4 us
  transfers between devices with their start and end apart: 12, of which 12 were waited for; matrix products, arithmetic and copies ran while one was open for 4% of the time, Pallas kernels for 0%

commit v1 on v0

v1 whole, which is shorter than its diff:
```python
import functools
import math
import jax
import jax.numpy as jnp
from jax import lax
from jax.experimental import pallas as pl
from jax.experimental.pallas import tpu as pltpu
from jax.sharding import Mesh, PartitionSpec as P

SEG = 48
HD = 128
GRP = 3
XN = 4
SN = 16
RUN = XN * SEG
NRUN = 4
CH = NRUN * RUN


def rms_norm(hidden, gain):
    hidden_f = hidden.astype(jnp.float32)
    inv_rms = lax.rsqrt(jnp.mean(hidden_f * hidden_f, axis=-1, keepdims=True) + 1e-5)
    return (hidden_f * inv_rms * gain.astype(jnp.float32)).astype(jnp.bfloat16)


def seg_positions(dev_ids, rows, dev_total):
    offset = jnp.arange(rows)
    half_len = rows // 2
    seg_idx = jnp.where(offset < half_len, dev_ids[..., None], 2 * dev_total - 1 - dev_ids[..., None])
    return seg_idx * half_len + offset % half_len


def flash_kernel(q_ref, kv_ref, o_ref):
    group = lax.axis_index('z') * 4 + lax.axis_index('y')
    scale = math.log2(math.e) / math.sqrt(HD)

    def quarter_block(quarter):
        return jnp.where(quarter == 0, 0, jnp.where(quarter == 1, 2, jnp.where(quarter == 2, 3, 1)))

    def one_quarter(quarter, carry):
        blk = quarter_block(quarter)
        desc = quarter >= 2
        order = quarter * SN + jnp.where(desc, SN - 1 - group, group)
        xs = [jnp.where(desc, XN - 1 - i, i) for i in range(XN)]
        qs = [jnp.concatenate([q_ref[x, blk, :, h * HD:(h + 1) * HD] for x in xs], axis=0) for h in range(GRP)]

        def chunk(c, state, masked):
            kq = c // (SN // NRUN)
            kblk = quarter_block(kq)
            kdesc = kq >= 2
            parts_k, parts_v = [], []
            for r in range(NRUN):
                idx = (c % (SN // NRUN)) * NRUN + r
                member = jnp.where(kdesc, SN - 1 - idx, idx)
                for i in range(XN):
                    x = jnp.where(kdesc, XN - 1 - i, i)
                    parts_k.append(kv_ref[member, x, kblk, :, :HD])
                    parts_v.append(kv_ref[member, x, kblk, :, HD:])
            keys = jnp.concatenate(parts_k, axis=0)
            vals = jnp.concatenate(parts_v, axis=0)
            out = []
            if masked:
                row = lax.broadcasted_iota(jnp.int32, (RUN, CH), 0)
                col = lax.broadcasted_iota(jnp.int32, (RUN, CH), 1)
                visible = col <= row + (order - c * NRUN) * RUN
            for h in range(GRP):
                m, l, acc = state[h]
                s = lax.dot_general(qs[h], keys, (((1,), (1,)), ((), ())), preferred_element_type=jnp.float32)
                if masked:
                    s = jnp.where(visible, s, -jnp.inf)
                m_new = jnp.maximum(m, jnp.max(s, axis=-1, keepdims=True))
                e = jnp.exp2((s - m_new) * scale)
                alpha = jnp.exp2((m - m_new) * scale)
                l_new = l * alpha + jnp.sum(e, axis=-1, keepdims=True)
                pv = jnp.dot(e.astype(jnp.bfloat16), vals, preferred_element_type=jnp.float32)
                out.append((m_new, l_new, acc * alpha + pv))
            return tuple(out)

        last = order // NRUN
        init = tuple((jnp.full((RUN, 1), -jnp.inf, jnp.float32), jnp.zeros((RUN, 1), jnp.float32),
                      jnp.zeros((RUN, HD), jnp.float32)) for _ in range(GRP))
        state = chunk(last, init, True)
        state = lax.fori_loop(0, last, lambda c, st: chunk(c, st, False), state)
        for h in range(GRP):
            m, l, acc = state[h]
            o = (acc / l).astype(jnp.bfloat16)
            for i in range(XN):
                o_ref[xs[i], blk, :, h * HD:(h + 1) * HD] = o[i * SEG:(i + 1) * SEG]
        return carry

    lax.fori_loop(0, 4, one_quarter, 0)


def flash(q, kv):
    return pl.pallas_call(
        flash_kernel,
        out_shape=jax.ShapeDtypeStruct(q.shape, jnp.bfloat16),
        in_specs=[pl.BlockSpec(memory_space=pltpu.VMEM)] * 2,
        out_specs=pl.BlockSpec(memory_space=pltpu.VMEM),
        compiler_params=pltpu.CompilerParams(vmem_limit_bytes=40 << 20),
        cost_estimate=pl.CostEstimate(flops=2 * 2 * 130 * 192 * 576 * 128, bytes_accessed=8 << 20, transcendentals=0),
        name='flash',
    )(q, kv)


def solution(mesh):
    tp_size = mesh.shape['tp']
    cp_size = mesh.shape['cp']
    dev_total = tp_size * cp_size
    mesh5 = Mesh(mesh.devices.reshape(1, tp_size, 4, 4, 4), ('dp', 'tp', 'z', 'y', 'x'))
    row_spec = P(('dp', 'tp', 'z', 'y', 'x'), None)
    gain_spec = P(None, None)
    q_spec = P(None, None, 'tp', None)
    col_spec = P(None, None, 'tp')
    o_spec = P(None, 'tp', None, None)
    down_spec = P(None, 'tp', None)

    def body(tokens, norm_attn, norm_mlp, w_q, w_k, w_v, w_o, w_gate, w_up, w_down):
        rows = tokens.shape[0]
        toks = tp_size * rows
        cp_idx = (lax.axis_index('z') * 4 + lax.axis_index('y')) * 4 + lax.axis_index('x')
        tp_devs = jnp.arange(tp_size) * cp_size + cp_idx
        pos = seg_positions(tp_devs, rows, dev_total).reshape(toks)
        inv_freq = 500000.0 ** (-(jnp.arange(HD // 2, dtype=jnp.float32) * 2.0 / HD))
        angles = pos.astype(jnp.float32)[:, None] * inv_freq[None, :]
        cos_a = jnp.cos(angles)[:, None, :]
        sin_a = jnp.sin(angles)[:, None, :]

        def rotary(v):
            a, b = v[..., :HD // 2], v[..., HD // 2:]
            return jnp.concatenate([a * cos_a - b * sin_a, b * cos_a + a * sin_a], axis=-1)

        hidden = tokens
        for layer in range(w_q.shape[0]):
            normed = lax.all_gather(rms_norm(hidden, norm_attn[layer]), 'tp', axis=0, tiled=True)
            q_proj = jnp.einsum('rd,dhe->rhe', normed, w_q[layer], preferred_element_type=jnp.float32)
            q = rotary(q_proj).astype(jnp.bfloat16).reshape(toks, XN, GRP * HD)
            k_proj = jnp.dot(normed, w_k[layer], preferred_element_type=jnp.float32)
            k = rotary(k_proj.reshape(toks, XN, HD)).astype(jnp.bfloat16)
            v = jnp.dot(normed, w_v[layer], preferred_element_type=jnp.float32).astype(jnp.bfloat16).reshape(toks, XN, HD)
            send = jnp.concatenate([q, k, v], axis=-1).transpose(1, 0, 2)
            got = lax.all_to_all(send, 'x', split_axis=0, concat_axis=0, tiled=True)
            q_own = got[:, :, :GRP * HD].reshape(XN, 4, SEG, GRP * HD)
            kv_own = got[:, :, GRP * HD:].reshape(XN, 4, SEG, 2 * HD)
            kv_all = lax.all_gather(kv_own, ('z', 'y'), axis=0, tiled=False)
            o_own = flash(q_own, kv_all.reshape(SN, XN, 4, SEG, 2 * HD))
            o = lax.all_to_all(o_own.reshape(XN, toks, GRP * HD), 'x', split_axis=0, concat_axis=0, tiled=True)
            attn_part = jnp.einsum('xre,xed->rd', o, w_o[layer].reshape(XN, GRP * HD, -1), preferred_element_type=jnp.float32)
            attn_out = lax.psum_scatter(attn_part, 'tp', scatter_dimension=0, tiled=True)
            hidden_mid = (hidden.astype(jnp.float32) + attn_out).astype(jnp.bfloat16)
            normed_mlp = lax.all_gather(rms_norm(hidden_mid, norm_mlp[layer]), 'tp', axis=0, tiled=True)
            gate = jnp.dot(normed_mlp, w_gate[layer], preferred_element_type=jnp.float32)
            up = jnp.dot(normed_mlp, w_up[layer], preferred_element_type=jnp.float32)
            act = (jax.nn.silu(gate) * up).astype(jnp.bfloat16)
            mlp_part = jnp.dot(act, w_down[layer], preferred_element_type=jnp.float32)
            mlp_out = lax.psum_scatter(mlp_part, 'tp', scatter_dimension=0, tiled=True)
            hidden = (hidden_mid.astype(jnp.float32) + mlp_out).astype(jnp.bfloat16)
        return hidden

    return jax.shard_map(
        body,
        mesh=mesh5,
        in_specs=(row_spec, gain_spec, gain_spec, q_spec, col_spec, col_spec, o_spec, col_spec, col_spec, down_spec),
        out_specs=row_spec,
        check_vma=False,
    )
```

time: 972 us -> 549 us (0.56)
  matrix products: 365 us -> 107 us
  waiting for transfers between devices: 441 us -> 217 us
  other arithmetic: 129 us -> 18.1 us
  Pallas kernels: 0 us -> 93.7 us
  blocking collectives: 0 us -> 48 us
  local copies, waits for them, and re-layouts: 16.2 us -> 45.9 us
    dot_general x28 -> x12, matrix products: 365 us -> 107 us  [the longest x2 41.3 us: body(): mlp_part = jnp.dot(act, w_down[layer], preferred_element_type=jnp.float32)]
    all_gather x8 -> x6, waiting for transfers between devices: 389 us -> 164 us  [the longest x2 122 us: body(): kv_all = lax.all_gather(kv_own, ('z', 'y'), axis=0, tiled=False)]
    reduce_sum x8 -> x0, other arithmetic: 105 us -> none  [one_block(): row_sum = jnp.sum(weights, axis=-1, keepdims=True)]
    pallas_call x0 -> x2, Pallas kernels: none -> 93.7 us  [flash(): pl.pallas_call(flash_kernel, out_shape=jax.ShapeDtypeStruct(q.shape, jnp....]
    all_to_all x0 -> x3, blocking collectives: none -> 48 us  [the longest x2 35.4 us: body(): got = lax.all_to_all(send, 'x', split_axis=0, concat_axis=0, tiled=True)]
    slice x0 -> x5, local copies, waits for them, and re-layouts: none -> 16.8 us  [the longest x1 15.1 us: body(): w_o[layer].reshape(XN, GRP * HD, -1)]
  transfers between devices with their start and end apart: 12 -> 11, of which waited for: 12 -> 10; matrix products, arithmetic and copies ran while one was open for 4% -> 5% of each run, Pallas kernels for 0% -> 0%
where the time goes in v1:
time: 549 us; the launch traced here: 548 us
  waiting for transfers between devices  217 us (40%)
  matrix products  107 us (19%)
  Pallas kernels  93.7 us (17%)
  blocking collectives  48 us (9%)
  local copies, waits for them, and re-layouts  45.9 us (8%)
  other arithmetic  18.1 us (3%)
  between operations  13.9 us (3%)
    all_gather x2, waiting for transfers between devices, body(): kv_all = lax.all_gather(kv_own, ('z', 'y'), axis=0, tiled=False)  122 us
    pallas_call x2, Pallas kernels, flash(): pl.pallas_call(flash_kernel, out_shape=jax.ShapeDtypeStruct(q.shape, jnp....  93.7 us
    dot_general x2, matrix products, body(): mlp_part = jnp.dot(act, w_down[layer], preferred_element_type=jnp.float32)  41.3 us
    all_to_all x2, blocking collectives, body(): got = lax.all_to_all(send, 'x', split_axis=0, concat_axis=0, tiled=True)  35.4 us
    dot_general x2, matrix products, body(): jnp.dot(normed_mlp, w_gate[layer], preferred_element_type=jnp.float32)  29.2 us
    reduce_scatter x2, waiting for transfers between devices, body(): mlp_out = lax.psum_scatter(mlp_part, 'tp', scatter_dimension=0, tiled=True)  27.4 us
    all_gather x2, waiting for transfers between devices, body(): lax.all_gather(rms_norm(hidden_mid, norm_mlp[layer]), 'tp', axis=0, tiled...  26.1 us
    reduce_scatter x2, waiting for transfers between devices, body(): lax.psum_scatter(attn_part, 'tp', scatter_dimension=0, tiled=True)  25 us
  transfers between devices with their start and end apart: 11, of which 10 were waited for; matrix products, arithmetic and copies ran while one was open for 5% of the time, Pallas kernels for 0%

profile of v1, /device:TPU:1, one launch (start us, length us, event | category | flops | bytes accessed | tf_op | source)
XLA Modules:
  0.0 548.2 jit_solution(16427637602656418396)
XLA Ops:
  20.5 5.9 %all-gather.7.cloned.1.call-done = bf16[192,3072]{1,0:T(8,128)(2,1)} async-done(((bf16[96,3072]{1,0:T(8,128)(2,1)}), bf16[192,3072]{1,0:T(8,128)(2,1)}) %all-gather.7.cloned.1.call-update) | async-done | bytes 1179664 | tf_op jit(solution)/shard_map/all_gather | solution.py:135
  26.4 6.0 %fusion.20 = f32[192,12,128]{2,0,1:T(8,128)S(1)} fusion(bf16[2,3072,12,128]{3,1,2,0:T(8,128)(2,1)} %param.13, bf16[192,3072]{1,0:T(8,128)(2,1)} %all-gather.7.cloned.1.call-done), kind=kOutput, calls=%fused_computation.20 | convolution fusion | flops 1811939328 | bytes 11796480 | tf_op jit(solution)/shard_map/rd,dhe->rhe/dot_general | solution.py:136
  44.3 17.7 %all_to_all.20 = bf16[4,192,640]{2,1,0:T(8,128)(2,1)S(1)} all-to-all(bf16[4,192,640]{2,1,0:T(8,128)(2,1)S(1)} %copy.31), channel_id=1, replica_groups=mesh['dp'=1,'tp'=2,'z'=4,'y'=4,'x'=4] {'x'}, dimensions={0} | all-to-all | bytes 1966080 | tf_op jit(solution)/shard_map/all_to_all | solution.py:142
  62.9 61.1 %all-gather.9.cloned.1.call-done.kv_ref = bf16[16,4,4,48,256]{4,3,2,1,0:T(8,128)(2,1)} async-done(((bf16[1,4,4,48,256]{4,3,2,1,0:T(8,128)(2,1)}), bf16[16,4,4,48,256]{4,3,2,1,0:T(8,128)(2,1)}) %all-gather.9.cloned.1.call-update) | async-done | bytes 6291472 | tf_op jit(solution)/shard_map/all_gather | solution.py:145
  126.8 47.3 %flash.2 = bf16[4,4,48,384]{3,2,1,0:T(8,128)(2,1)} custom-call(bf16[4,4,48,384]{3,2,1,0:T(8,128)(2,1)S(1)} %bitcast.98, bf16[16,4,4,48,256]{4,3,2,1,0:T(8,128)(2,1)S(1)} %copy-done.1), custom_call_target="tpu_custom_call" | custom-call | flops 7361003520 | bytes 8388608 | tf_op jit(solution)/shard_map/flash/pallas_call | solution.py:95
  178.0 15.1 %fusion.91 = (bf16[1,12,128,3072]{3,2,1,0:T(8,128)(2,1)}, bf16[1,12,128,3072]{3,2,1,0:T(8,128)(2,1)}) fusion(bf16[2,12,128,3072]{3,2,1,0:T(8,128)(2,1)} %param.16), kind=kLoop, calls=%fused_computation.116 | loop fusion | bytes 37748736 | tf_op jit(solution)/shard_map/slice | solution.py:148
  193.1 7.1 %convolution_bitcast_fusion.1 = f32[192,3072]{1,0:T(8,128)} fusion(bf16[4,192,384]{2,1,0:T(8,128)(2,1)S(1)} %all-to-all-done.1, bf16[4,384,3072]{2,1,0:T(8,128)(2,1)} %bitcast.102), kind=kOutput, calls=%fused_computation.29 | convolution fusion | flops 1811939328 | bytes 12386304 | tf_op jit(solution)/shard_map/xre,xed->rd/dot_general | solution.py:148
  200.9 12.8 %reduce-scatter.5.cloned.1.call-done = f32[96,3072]{1,0:T(8,128)} async-done(((f32[192,3072]{1,0:T(8,128)}), f32[96,3072]{1,0:T(8,128)}) %reduce-scatter.5.cloned.1.call-update) | async-done | bytes 1179664 | tf_op jit(solution)/shard_map/reduce_scatter | solution.py:149
  216.4 13.2 %all-gather.11.cloned.1.call-done = bf16[192,3072]{1,0:T(8,128)(2,1)} async-done(((bf16[96,3072]{1,0:T(8,128)(2,1)}), bf16[192,3072]{1,0:T(8,128)(2,1)}) %all-gather.11.cloned.1.call-update) | async-done | bytes 1179664 | tf_op jit(solution)/shard_map/all_gather | solution.py:151
  229.6 14.6 %fusion.10 = f32[192,4096]{1,0:T(8,128)} fusion(bf16[192,3072]{1,0:T(8,128)(2,1)} %all-gather.11.cloned.1.call-done, bf16[2,3072,4096]{2,1,0:T(8,128)(2,1)} %param.17), kind=kOutput, calls=%fused_computation.10 | convolution fusion | flops 4831838208 | bytes 29491200 | tf_op jit(solution)/shard_map/dot_general | solution.py:152
  244.3 20.6 %fusion.6 = f32[192,3072]{1,0:T(8,128)} fusion(bf16[2,4096,3072]{2,1,0:T(8,128)(2,1)} %param.19, bf16[192,3072]{1,0:T(8,128)(2,1)S(1)} %copy-done.10, bf16[2,3072,4096]{2,1,0:T(8,128)(2,1)} %param.18, f32[192,4096]{1,0:T(8,128)} %fusion.10), kind=kOutput, calls=%fused_computation.6 | convolution fusion | flops 9668395008 | bytes 57016320 | tf_op jit(solution)/shard_map/dot_general | solution.py:155
  265.0 13.7 %reduce-scatter.7.cloned.1.call-done = f32[96,3072]{1,0:T(8,128)} async-done(((f32[192,3072]{1,0:T(8,128)}), f32[96,3072]{1,0:T(8,128)}) %reduce-scatter.7.cloned.1.call-update) | async-done | bytes 1179664 | tf_op jit(solution)/shard_map/reduce_scatter | solution.py:156
  285.5 9.8 %all-gather.13.cloned.1.call-done = bf16[192,3072]{1,0:T(8,128)(2,1)} async-done(((bf16[96,3072]{1,0:T(8,128)(2,1)}), bf16[192,3072]{1,0:T(8,128)(2,1)}) %all-gather.13.cloned.1.call-update) | async-done | bytes 1179664 | tf_op jit(solution)/shard_map/all_gather | solution.py:135
  295.3 6.0 %fusion.18 = f32[192,12,128]{2,0,1:T(8,128)S(1)} fusion(bf16[2,3072,12,128]{3,1,2,0:T(8,128)(2,1)} %param.13, bf16[192,3072]{1,0:T(8,128)(2,1)} %all-gather.13.cloned.1.call-done), kind=kOutput, calls=%fused_computation.18 | convolution fusion | flops 1811939328 | bytes 11796480 | tf_op jit(solution)/shard_map/rd,dhe->rhe/dot_general | solution.py:136
  313.3 17.7 %all_to_all.21 = bf16[4,192,640]{2,1,0:T(8,128)(2,1)S(1)} all-to-all(bf16[4,192,640]{2,1,0:T(8,128)(2,1)S(1)} %copy.36), channel_id=1, replica_groups=mesh['dp'=1,'tp'=2,'z'=4,'y'=4,'x'=4] {'x'}, dimensions={0} | all-to-all | bytes 1966080 | tf_op jit(solution)/shard_map/all_to_all | solution.py:142
  331.9 61.1 %all-gather.15.cloned.1.call-done.kv_ref = bf16[16,4,4,48,256]{4,3,2,1,0:T(8,128)(2,1)} async-done(((bf16[1,4,4,48,256]{4,3,2,1,0:T(8,128)(2,1)}), bf16[16,4,4,48,256]{4,3,2,1,0:T(8,128)(2,1)}) %all-gather.15.cloned.1.call-update) | async-done | bytes 6291472 | tf_op jit(solution)/shard_map/all_gather | solution.py:145
  395.7 46.5 %flash.3 = bf16[4,4,48,384]{3,2,1,0:T(8,128)(2,1)S(1)} custom-call(bf16[4,4,48,384]{3,2,1,0:T(8,128)(2,1)S(1)} %bitcast.99, bf16[16,4,4,48,256]{4,3,2,1,0:T(8,128)(2,1)S(1)} %copy-done), custom_call_target="tpu_custom_call" | custom-call | flops 7361003520 | bytes 8388608 | tf_op jit(solution)/shard_map/flash/pallas_call | solution.py:95
  442.2 12.7 %all_to_all.22 = bf16[4,192,384]{2,1,0:T(8,128)(2,1)S(1)} all-to-all(bf16[4,192,384]{2,1,0:T(8,128)(2,1)S(1)} %bitcast.100), channel_id=1, replica_groups=mesh['dp'=1,'tp'=2,'z'=4,'y'=4,'x'=4] {'x'}, dimensions={0} | all-to-all | bytes 1179648 | tf_op jit(solution)/shard_map/all_to_all | solution.py:147
  454.9 7.2 %convolution_bitcast_fusion = f32[192,3072]{1,0:T(8,128)} fusion(bf16[4,192,384]{2,1,0:T(8,128)(2,1)S(1)} %all_to_all.22, bf16[4,384,3072]{2,1,0:T(8,128)(2,1)} %bitcast.101), kind=kOutput, calls=%fused_computation.28 | convolution fusion | flops 1811939328 | bytes 12386304 | tf_op jit(solution)/shard_map/xre,xed->rd/dot_general | solution.py:148
  462.2 12.2 %reduce-scatter.9.cloned.1.call-done = f32[96,3072]{1,0:T(8,128)} async-done(((f32[192,3072]{1,0:T(8,128)}), f32[96,3072]{1,0:T(8,128)}) %reduce-scatter.9.cloned.1.call-update) | async-done | bytes 1179664 | tf_op jit(solution)/shard_map/reduce_scatter | solution.py:149
  477.3 12.9 %all-gather.17.cloned.1.call-done = bf16[192,3072]{1,0:T(8,128)(2,1)} async-done(((bf16[96,3072]{1,0:T(8,128)(2,1)}), bf16[192,3072]{1,0:T(8,128)(2,1)}) %all-gather.17.cloned.1.call-update) | async-done | bytes 1179664 | tf_op jit(solution)/shard_map/all_gather | solution.py:151
  490.2 14.5 %fusion.4 = f32[192,4096]{1,0:T(8,128)} fusion(bf16[192,3072]{1,0:T(8,128)(2,1)} %all-gather.17.cloned.1.call-done, bf16[2,3072,4096]{2,1,0:T(8,128)(2,1)} %param.17), kind=kOutput, calls=%fused_computation.4 | convolution fusion | flops 4831838208 | bytes 29491200 | tf_op jit(solution)/shard_map/dot_general | solution.py:152
  504.8 20.7 %fusion = f32[192,3072]{1,0:T(8,128)} fusion(bf16[2,4096,3072]{2,1,0:T(8,128)(2,1)} %param.19, bf16[192,3072]{1,0:T(8,128)(2,1)S(1)} %copy-done.11, bf16[2,3072,4096]{2,1,0:T(8,128)(2,1)} %param.18, f32[192,4096]{1,0:T(8,128)} %fusion.4), kind=kOutput, calls=%fused_computation | convolution fusion | flops 9668395008 | bytes 57016320 | tf_op jit(solution)/shard_map/dot_general | solution.py:155
  525.5 13.7 %reduce-scatter.11.cloned.1.call-done = f32[96,3072]{1,0:T(8,128)} async-done(((f32[192,3072]{1,0:T(8,128)}), f32[96,3072]{1,0:T(8,128)}) %reduce-scatter.11.cloned.1.call-update) | async-done | bytes 1179664 | tf_op jit(solution)/shard_map/reduce_scatter | solution.py:156
  (99 shorter events, 64.2 us)
Async XLA Ops:
  6.5 19.8 %all-gather.7.cloned.1.call-start = ((), (), s32[]{:S(2)}) async-start(), calls=%async_computation.8 | async-start | bytes 1769472 | tf_op jit(solution)/shard_map/all_gather | solution.py:135
  10.8 113.3 %all-gather.9.cloned.1.call-start = ((), (), s32[]{:S(2)}) async-start(), calls=%async_computation.9 | async-start | bytes 6684672 | tf_op jit(solution)/shard_map/all_gather | solution.py:145
  39.4 1.3 copy-start.7
  40.7 2.8 copy-start.6
  124.0 2.8 copy-start.1
  174.1 19.1 %all-to-all-start.1 = ((bf16[4,192,384]{2,1,0:T(8,128)(2,1)}), bf16[4,192,384]{2,1,0:T(8,128)(2,1)S(1)}, u32[]{:S(2)}, u32[]{:S(2)}) async-start(bf16[4,192,384]{2,1,0:T(8,128)(2,1)} %bitcast.10), calls=%async_computation.1 | async-start | bytes 1179648 | tf_op jit(solution)/shard_map/all_to_all | solution.py:147
  178.0 35.7 %reduce-scatter.5.cloned.1.call-start = ((), (), s32[]{:S(2)}) async-start(), calls=%async_computation.10 | async-start | bytes 3538944 | tf_op jit(solution)/shard_map/reduce_scatter | solution.py:149
  200.2 0.7 copy-start.9
  200.2 13.6 %copy-start.4 = (bf16[96,3072]{1,0:T(8,128)(2,1)S(1)}, bf16[96,3072]{1,0:T(8,128)(2,1)}, u32[]{:S(2)}) copy-start(bf16[96,3072]{1,0:T(8,128)(2,1)} %param.10) | copy-start | bytes 1769476
  200.2 29.4 %all-gather.11.cloned.1.call-start = ((), (), s32[]{:S(2)}) async-start(), calls=%async_computation.11 | async-start | bytes 1769472 | tf_op jit(solution)/shard_map/all_gather | solution.py:151
  216.4 62.2 %reduce-scatter.7.cloned.1.call-start = ((), (), s32[]{:S(2)}) async-start(), calls=%async_computation.12 | async-start | bytes 3538944 | tf_op jit(solution)/shard_map/reduce_scatter | solution.py:156
  229.6 14.6 %copy-start.10 = (bf16[192,3072]{1,0:T(8,128)(2,1)S(1)}, bf16[192,3072]{1,0:T(8,128)(2,1)}, u32[]{:S(2)}) copy-start(bf16[192,3072]{1,0:T(8,128)(2,1)} %all-gather.11.cloned.1.call-done) | copy-start | bytes 3538948
  264.9 30.4 %all-gather.13.cloned.1.call-start = ((), (), s32[]{:S(2)}) async-start(), calls=%async_computation.13 | async-start | bytes 1769472 | tf_op jit(solution)/shard_map/all_gather | solution.py:135
  280.2 0.8 copy-start.2
  282.1 110.9 %all-gather.15.cloned.1.call-start = ((), (), s32[]{:S(2)}) async-start(), calls=%async_computation.14 | async-start | bytes 6684672 | tf_op jit(solution)/shard_map/all_gather | solution.py:145
  308.4 1.3 copy-start.8
  309.6 2.8 copy-start.5
  331.7 142.6 %reduce-scatter.9.cloned.1.call-start = ((), (), s32[]{:S(2)}) async-start(), calls=%async_computation.15 | async-start | bytes 3538944 | tf_op jit(solution)/shard_map/reduce_scatter | solution.py:149
  393.0 2.8 copy-start
  462.1 12.2 %copy-start.3 = (bf16[96,3072]{1,0:T(8,128)(2,1)S(1)}, bf16[96,3072]{1,0:T(8,128)(2,1)}, u32[]{:S(2)}) copy-start(bf16[96,3072]{1,0:T(8,128)(2,1)} %copy-done.2) | copy-start | bytes 1769476
  462.1 28.1 %all-gather.17.cloned.1.call-start = ((), (), s32[]{:S(2)}) async-start(), calls=%async_computation.16 | async-start | bytes 1769472 | tf_op jit(solution)/shard_map/all_gather | solution.py:151
  477.0 62.2 %reduce-scatter.11.cloned.1.call-start = ((), (), s32[]{:S(2)}) async-start(), calls=%async_computation.17 | async-start | bytes 3538944 | tf_op jit(solution)/shard_map/reduce_scatter | solution.py:156
  490.2 14.6 %copy-start.11 = (bf16[192,3072]{1,0:T(8,128)(2,1)S(1)}, bf16[192,3072]{1,0:T(8,128)(2,1)}, u32[]{:S(2)}) copy-start(bf16[192,3072]{1,0:T(8,128)(2,1)} %all-gather.17.cloned.1.call-done) | copy-start | bytes 3538948
Sparse Core Ops, SparseCore 0:
  10.9 15.4 all-gather.6
  62.9 61.0 all-gather.8
  200.4 13.3 reduce-scatter.4
  216.5 13.0 all-gather.10
  265.1 13.5 reduce-scatter.6
  282.2 13.0 all-gather.12
  331.9 61.0 all-gather.14
  462.2 12.0 reduce-scatter.8
  477.1 13.0 all-gather.16
  525.6 13.5 reduce-scatter.10

commit v2 on v1

v2 whole, which is shorter than its diff:
```python
import functools
import math
import jax
import jax.numpy as jnp
from jax import lax
from jax.experimental import pallas as pl
from jax.experimental.pallas import tpu as pltpu
from jax.sharding import Mesh, PartitionSpec as P

def rms_norm(hidden, gain):
    hidden_f = hidden.astype(jnp.float32)
    inv_rms = lax.rsqrt(jnp.mean(hidden_f * hidden_f, axis=-1, keepdims=True) + 1e-5)
    return (hidden_f * inv_rms * gain.astype(jnp.float32)).astype(jnp.bfloat16)


def seg_positions(dev_ids, rows, dev_total):
    offset = jnp.arange(rows)
    half_len = rows // 2
    seg_idx = jnp.where(offset < half_len, dev_ids[..., None], 2 * dev_total - 1 - dev_ids[..., None])
    return seg_idx * half_len + offset % half_len


SEG = 48
HD = 128
GRP = 3
XN = 4
SN = 16
RUN = XN * SEG
NRUN = 4
CH = NRUN * RUN
QR = GRP * RUN
TOK = 192
SCALE = math.log2(math.e) / math.sqrt(HD)
NB = 20


def quarter_block(quarter):
    return jnp.where(quarter == 0, 0, jnp.where(quarter == 1, 2, jnp.where(quarter == 2, 3, 1)))


def attn_kernel(q_send, kv_send, o_out, q_own, kv_all, o_own, o_recv, s_a, s_b, mx_a, mx_b, m_ref, l_ref, acc_ref,
                send_a, recv_a, send_b, recv_b, send_o, recv_o, local_sem):
    zi, yi, xi = lax.axis_index('z'), lax.axis_index('y'), lax.axis_index('x')
    group = zi * 4 + yi

    def slot(coords):
        return coords[0] * 4 + coords[1]

    def plus(v, d):
        return lax.rem(v + d + 4, 4)

    barrier = pltpu.get_barrier_semaphore()
    for d in (1, 2, 3):
        pl.semaphore_signal(barrier, inc=1, device_id={'x': plus(xi, d)}, device_id_type=pl.DeviceIdType.MESH)
    for d in (1, -1):
        pl.semaphore_signal(barrier, inc=1, device_id={'y': plus(yi, d)}, device_id_type=pl.DeviceIdType.MESH)
        pl.semaphore_signal(barrier, inc=1, device_id={'z': plus(zi, d)}, device_id_type=pl.DeviceIdType.MESH)
    own_q = pltpu.make_async_copy(q_send.at[xi], q_own.at[xi], local_sem.at[0])
    own_kv = pltpu.make_async_copy(kv_send.at[xi], kv_all.at[group, xi], local_sem.at[1])
    own_q.start()
    own_kv.start()
    pl.semaphore_wait(barrier, 7)

    def remote(src, dst, ssem, rsem, dev):
        return pltpu.make_async_remote_copy(src_ref=src, dst_ref=dst, send_sem=ssem, recv_sem=rsem, device_id=dev,
                                            device_id_type=pl.DeviceIdType.MESH)

    kv_msgs, q_msgs = [], []
    for d in (1, 2, 3):
        to = plus(xi, d)
        kv_msgs.append(remote(kv_send.at[to], kv_all.at[group, xi], send_a.at[d - 1], recv_a.at[d - 1], {'x': to}))
        q_msgs.append(remote(q_send.at[to], q_own.at[xi], send_a.at[d + 2], recv_a.at[d + 2], {'x': to}))
    for c in kv_msgs:
        c.start()
    for c in q_msgs:
        c.start()
    own_kv.wait()
    for c in kv_msgs:
        c.wait_recv()

    pos = (zi, yi)
    names = ('z', 'y')

    def at(axis, da, db):
        other = 1 - axis
        c = [None, None]
        c[axis] = plus(pos[axis], da)
        c[other] = plus(pos[other], db)
        return slot(c)

    def msg(half, idx, where, part, axis, d):
        base = half * 2
        lo, n = (base, 2) if part is None else (base + part, 1)
        ref = kv_all.at[where, pl.ds(lo, n)]
        k = half * NB + idx
        return remote(ref, ref, send_b.at[k], recv_b.at[k], {names[axis]: plus(pos[axis], d)})

    first = (1, 0)
    stage = [dict() for _ in range(2)]
    offs = (0, -1, 1, 2)

    def begin(half, key, m):
        stage[half][key] = m
        m.start()

    def send_second(half, j):
        a = first[half]
        b = 1 - a
        for s, d in enumerate((1, -1)):
            begin(half, ('b', j, d), msg(half, 4 + j * 4 + s, at(a, offs[j], 0), None, b, d))

    def forward_second(half, j):
        a = first[half]
        b = 1 - a
        for s, d in enumerate((1, -1)):
            stage[half][('b', j, d)].wait_recv()
            begin(half, ('f', j, d), msg(half, 4 + j * 4 + 2 + s, at(a, offs[j], -d), s, b, d))

    for half in range(2):
        a = first[half]
        for s, d in enumerate((1, -1)):
            begin(half, ('a', d), msg(half, s, group, None, a, d))
    for half in range(2):
        send_second(half, 0)
    for half in range(2):
        a = first[half]
        for s, d in enumerate((1, -1)):
            stage[half][('a', d)].wait_recv()
            begin(half, ('g', d), msg(half, 2 + s, at(a, -d, 0), s, a, d))
    for half in range(2):
        send_second(half, 1)
        send_second(half, 2)
    for half in range(2):
        forward_second(half, 0)
    for half in range(2):
        for d in (1, -1):
            stage[half][('g', d)].wait_recv()
        send_second(half, 3)
    for j in (1, 2, 3):
        for half in range(2):
            forward_second(half, j)
    own_q.wait()
    for c in q_msgs:
        c.wait_recv()
    for half in range(2):
        for j in range(4):
            for d in (1, -1):
                stage[half][('f', j, d)].wait_recv()

    def flash_quarter(step, carry):
        quarter = 3 - step
        blk = quarter_block(quarter)
        row0 = pl.multiple_of(blk * SEG, 16)
        desc = quarter >= 2
        order = quarter * SN + jnp.where(desc, SN - 1 - group, group)
        last = order // NRUN
        xs = [jnp.where(desc, XN - 1 - i, i) for i in range(XN)]
        qs = jnp.concatenate([q_own[x, h, pl.ds(row0, SEG), :] for h in range(GRP) for x in xs], axis=0)

        def load(c, which):
            kq = c // (SN // NRUN)
            krow = pl.multiple_of(quarter_block(kq) * SEG, 16)
            kdesc = kq >= 2
            parts = []
            for r in range(NRUN):
                idx = (c % (SN // NRUN)) * NRUN + r
                member = jnp.where(kdesc, SN - 1 - idx, idx)
                for i in range(XN):
                    x = jnp.where(kdesc, XN - 1 - i, i)
                    parts.append(kv_all[member, x, which, pl.ds(krow, SEG), :])
            return jnp.concatenate(parts, axis=0)

        def qk(c, s_ref, mx_ref, masked):
            s = lax.dot_general(qs, load(c, 0), (((1,), (1,)), ((), ())), preferred_element_type=jnp.float32)
            if masked:
                row = lax.broadcasted_iota(jnp.int32, (RUN, CH), 0)
                col = lax.broadcasted_iota(jnp.int32, (RUN, CH), 1)
                visible = col <= row + (order - c * NRUN) * RUN
                s = jnp.concatenate([jnp.where(visible, s[h * RUN:(h + 1) * RUN], -jnp.inf) for h in range(GRP)], axis=0)
            s_ref[...] = s
            mx_ref[...] = jnp.broadcast_to(jnp.max(s, axis=-1, keepdims=True), (QR, HD))

        def soft(c, s_ref, mx_ref, valid):
            vals = load(c, 1)
            for h in range(GRP):
                rows = pl.ds(h * RUN, RUN)
                m_old = m_ref[rows, :]
                mx = mx_ref[rows, :]
                if valid is not None:
                    mx = jnp.where(valid, mx, -jnp.inf)
                m_new = jnp.maximum(m_old, mx)
                alpha = jnp.exp2((m_old - m_new) * SCALE)
                bias = m_new * SCALE
                if valid is not None:
                    bias = jnp.where(valid, bias, jnp.inf)
                lsum = l_ref[rows, :] * alpha
                es = []
                for t in range(CH // HD):
                    e = jnp.exp2(s_ref[rows, t * HD:(t + 1) * HD] * SCALE - bias)
                    lsum = lsum + e
                    es.append(e.astype(jnp.bfloat16))
                pv = jnp.dot(jnp.concatenate(es, axis=1), vals, preferred_element_type=jnp.float32)
                acc_ref[rows, :] = acc_ref[rows, :] * alpha + pv
                l_ref[rows, :] = lsum
                m_ref[rows, :] = m_new

        m_ref[...] = jnp.full((QR, HD), -jnp.inf, jnp.float32)
        l_ref[...] = jnp.zeros((QR, HD), jnp.float32)
        acc_ref[...] = jnp.zeros((QR, HD), jnp.float32)
        qk(last, s_a, mx_a, True)

        def pair(p, carry):
            c_cur = jnp.where(p == 0, last, 2 * p - 1)
            c_b = jnp.minimum(2 * p, last)
            c_a = jnp.minimum(2 * p + 1, last)
            qk(c_b, s_b, mx_b, False)
            soft(c_cur, s_a, mx_a, None)
            qk(c_a, s_a, mx_a, False)
            soft(c_b, s_b, mx_b, 2 * p < last)
            return carry

        lax.fori_loop(0, (last + 2) // 2, pair, 0)
        for h in range(GRP):
            rows = pl.ds(h * RUN, RUN)
            o = (acc_ref[rows, :] / jnp.sum(l_ref[rows, :], axis=-1, keepdims=True)).astype(jnp.bfloat16)
            for i in range(XN):
                o_own[xs[i], blk, h, :, :] = o[i * SEG:(i + 1) * SEG]
        for d in (1, 2, 3):
            to = plus(xi, d)
            remote(o_own.at[to, blk], o_recv.at[xi, blk], send_o.at[step, d - 1], recv_o.at[step, d - 1], {'x': to}).start()
        return carry

    lax.fori_loop(0, 4, flash_quarter, 0)
    o_recv[xi] = o_own[xi]
    for step in range(4):
        blk = (1, 3, 2, 0)[step]
        for d in (1, 2, 3):
            to = plus(xi, d)
            c = remote(o_own.at[to, blk], o_recv.at[xi, blk], send_o.at[step, d - 1], recv_o.at[step, d - 1], {'x': to})
            c.wait_send()
            c.wait_recv()
    o_out[...] = o_recv[...]
    for c in kv_msgs + q_msgs:
        c.wait_send()
    for half in range(2):
        for c in stage[half].values():
            c.wait_send()


def attention(q_send, kv_send):
    f32 = jnp.float32
    bf16 = jnp.bfloat16
    return pl.pallas_call(
        attn_kernel,
        out_shape=jax.ShapeDtypeStruct((XN, 4, GRP, SEG, HD), bf16),
        in_specs=[pl.BlockSpec(memory_space=pltpu.HBM)] * 2,
        out_specs=pl.BlockSpec(memory_space=pltpu.VMEM),
        scratch_shapes=[
            pltpu.VMEM((XN, GRP, TOK, HD), bf16),
            pltpu.VMEM((SN, XN, 2, TOK, HD), bf16),
            pltpu.VMEM((XN, 4, GRP, SEG, HD), bf16),
            pltpu.VMEM((XN, 4, GRP, SEG, HD), bf16),
            pltpu.VMEM((QR, CH), f32),
            pltpu.VMEM((QR, CH), f32),
            pltpu.VMEM((QR, HD), f32),
            pltpu.VMEM((QR, HD), f32),
            pltpu.VMEM((QR, HD), f32),
            pltpu.VMEM((QR, HD), f32),
            pltpu.VMEM((QR, HD), f32),
            pltpu.SemaphoreType.DMA((6,)),
            pltpu.SemaphoreType.DMA((6,)),
            pltpu.SemaphoreType.DMA((2 * NB,)),
            pltpu.SemaphoreType.DMA((2 * NB,)),
            pltpu.SemaphoreType.DMA((4, 3)),
            pltpu.SemaphoreType.DMA((4, 3)),
            pltpu.SemaphoreType.DMA((2,)),
        ],
        compiler_params=pltpu.CompilerParams(vmem_limit_bytes=40 << 20, collective_id=1, has_side_effects=True),
        cost_estimate=pl.CostEstimate(flops=2 * 2 * 130 * 192 * 576 * 128, bytes_accessed=8 << 20, transcendentals=0),
        name='attn',
    )(q_send, kv_send)


def solution(mesh):
    tp_size = mesh.shape['tp']
    cp_size = mesh.shape['cp']
    dev_total = tp_size * cp_size
    mesh5 = Mesh(mesh.devices.reshape(1, tp_size, 4, 4, 4), ('dp', 'tp', 'z', 'y', 'x'))
    row_spec = P(('dp', 'tp', 'z', 'y', 'x'), None)
    gain_spec = P(None, None)
    q_spec = P(None, None, 'tp', None)
    col_spec = P(None, None, 'tp')
    o_spec = P(None, 'tp', None, None)
    down_spec = P(None, 'tp', None)

    def body(tokens, norm_attn, norm_mlp, w_q, w_k, w_v, w_o, w_gate, w_up, w_down):
        rows = tokens.shape[0]
        toks = tp_size * rows
        cp_idx = (lax.axis_index('z') * 4 + lax.axis_index('y')) * 4 + lax.axis_index('x')
        tp_devs = jnp.arange(tp_size) * cp_size + cp_idx
        pos = seg_positions(tp_devs, rows, dev_total).reshape(toks)
        inv_freq = 500000.0 ** (-(jnp.arange(HD // 2, dtype=jnp.float32) * 2.0 / HD))
        angles = pos.astype(jnp.float32)[:, None] * inv_freq[None, :]
        cos_a = jnp.cos(angles)[None]
        sin_a = jnp.sin(angles)[None]

        def rotary(v):
            a, b = v[..., :HD // 2], v[..., HD // 2:]
            return jnp.concatenate([a * cos_a - b * sin_a, b * cos_a + a * sin_a], axis=-1)

        hidden = tokens
        for layer in range(w_q.shape[0]):
            normed = lax.all_gather(rms_norm(hidden, norm_attn[layer]), 'tp', axis=0, tiled=True)
            q_proj = jnp.einsum('rd,dhe->hre', normed, w_q[layer], preferred_element_type=jnp.float32)
            q_send = rotary(q_proj).astype(jnp.bfloat16).reshape(XN, GRP, toks, HD)
            k_proj = jnp.einsum('rd,dhe->hre', normed, w_k[layer].reshape(-1, XN, HD), preferred_element_type=jnp.float32)
            v_proj = jnp.einsum('rd,dhe->hre', normed, w_v[layer].reshape(-1, XN, HD), preferred_element_type=jnp.float32)
            kv_send = jnp.stack([rotary(k_proj).astype(jnp.bfloat16), v_proj.astype(jnp.bfloat16)], axis=1)
            o = attention(q_send, kv_send)
            o = o.transpose(1, 3, 0, 2, 4).reshape(toks, XN * GRP * HD)
            attn_part = jnp.dot(o, w_o[layer].reshape(XN * GRP * HD, -1), preferred_element_type=jnp.float32)
            attn_out = lax.psum_scatter(attn_part, 'tp', scatter_dimension=0, tiled=True)
            hidden_mid = (hidden.astype(jnp.float32) + attn_out).astype(jnp.bfloat16)
            normed_mlp = lax.all_gather(rms_norm(hidden_mid, norm_mlp[layer]), 'tp', axis=0, tiled=True)
            gate = jnp.dot(normed_mlp, w_gate[layer], preferred_element_type=jnp.float32)
            up = jnp.dot(normed_mlp, w_up[layer], preferred_element_type=jnp.float32)
            act = (jax.nn.silu(gate) * up).astype(jnp.bfloat16)
            mlp_part = jnp.dot(act, w_down[layer], preferred_element_type=jnp.float32)
            mlp_out = lax.psum_scatter(mlp_part, 'tp', scatter_dimension=0, tiled=True)
            hidden = (hidden_mid.astype(jnp.float32) + mlp_out).astype(jnp.bfloat16)
        return hidden

    return jax.shard_map(
        body,
        mesh=mesh5,
        in_specs=(row_spec, gain_spec, gain_spec, q_spec, col_spec, col_spec, o_spec, col_spec, col_spec, down_spec),
        out_specs=row_spec,
        check_vma=False,
    )
```

time: 549 us -> 429 us (0.78)
  waiting for transfers between devices: 217 us -> 89.9 us
  Pallas kernels: 93.7 us -> 159 us
  blocking collectives: 48 us -> 0 us
    all_gather x2 -> x0, waiting for transfers between devices: 122 us -> none  [body(): kv_all = lax.all_gather(kv_own, ('z', 'y'), axis=0, tiled=False)]
    pallas_call x2, Pallas kernels: 93.7 us -> 159 us  [attention(): pl.pallas_call(attn_kernel, out_shape=jax.ShapeDtypeStruct((XN, 4, GRP, S...]
    all_to_all x3 -> x0, blocking collectives: 48 us -> none  [the longest x2 35.4 us: body(): got = lax.all_to_all(send, 'x', split_axis=0, concat_axis=0, tiled=True)]
    dot_general x3 -> x0, local copies, waits for them, and re-layouts: 12.2 us -> none  [body(): k_proj = jnp.dot(normed, w_k[layer], preferred_element_type=jnp.float32)]
    slice x5 -> x3, local copies, waits for them, and re-layouts: 16.8 us -> 26 us  [the longest x1 15.1 us: body(): w_o[layer].reshape(XN * GRP * HD, -1)]
    all_gather x2, waiting for transfers between devices: 15.7 us -> 6.97 us  [body(): lax.all_gather(rms_norm(hidden, norm_attn[layer]), 'tp', axis=0, tiled=True)]
    unnamed x24, local copies, waits for them, and re-layouts: 8.49 us -> 14.6 us
  transfers between devices with their start and end apart: 11 -> 8, of which waited for: 10 -> 7; matrix products, arithmetic and copies ran while one was open for 5% -> 9% of each run, Pallas kernels for 0% -> 0%
where the time goes in v2:
time: 429 us; the launch traced here: 428 us
  Pallas kernels  159 us (37%)
  matrix products  106 us (25%)
  waiting for transfers between devices  89.9 us (21%)
  local copies, waits for them, and re-layouts  42.4 us (10%)
  other arithmetic  17.1 us (4%)
  between operations  13.8 us (3%)
    pallas_call x2, Pallas kernels, attention(): pl.pallas_call(attn_kernel, out_shape=jax.ShapeDtypeStruct((XN, 4, GRP, S...  159 us
    dot_general x2, matrix products, body(): mlp_part = jnp.dot(act, w_down[layer], preferred_element_type=jnp.float32)  41.3 us
    dot_general x2, matrix products, body(): jnp.dot(normed_mlp, w_gate[layer], preferred_element_type=jnp.float32)  29.3 us
    reduce_scatter x2, waiting for transfers between devices, body(): lax.psum_scatter(attn_part, 'tp', scatter_dimension=0, tiled=True)  29.3 us
    reduce_scatter x2, waiting for transfers between devices, body(): mlp_out = lax.psum_scatter(mlp_part, 'tp', scatter_dimension=0, tiled=True)  27.4 us
    all_gather x2, waiting for transfers between devices, body(): lax.all_gather(rms_norm(hidden_mid, norm_mlp[layer]), 'tp', axis=0, tiled...  26.2 us
    slice x1, local copies, waits for them, and re-layouts, body(): w_o[layer].reshape(XN * GRP * HD, -1)  15.1 us
    unnamed x24, local copies, waits for them, and re-layouts  14.6 us
  transfers between devices with their start and end apart: 8, of which 7 were waited for; matrix products, arithmetic and copies ran while one was open for 9% of the time, Pallas kernels for 0%

profile of v2, /device:TPU:1, one launch (start us, length us, event | category | flops | bytes accessed | tf_op | source)
XLA Modules:
  0.0 428.2 jit_solution(10422124047929542159)
XLA Ops:
  11.0 5.0 %fusion.104 = (bf16[1,3072,512]{2,1,0:T(8,128)(2,1)}, bf16[1,3072,512]{2,1,0:T(8,128)(2,1)S(1)}) fusion(bf16[2,3072,512]{2,1,0:T(8,128)(2,1)} %param.14), kind=kLoop, calls=%fused_computation.119 | loop fusion | bytes 12582912 | tf_op jit(solution)/shard_map/slice | solution.py:316
  19.1 5.9 %fusion.105 = (bf16[1,3072,512]{2,1,0:T(8,128)(2,1)}, bf16[1,3072,512]{2,1,0:T(8,128)(2,1)}) fusion(bf16[2,3072,512]{2,1,0:T(8,128)(2,1)} %param.15), kind=kLoop, calls=%fused_computation.120 | loop fusion | bytes 12582912 | tf_op jit(solution)/shard_map/slice | solution.py:317
  25.0 3.2 copy.30
  28.7 15.1 %fusion.103 = (bf16[1,12,128,3072]{3,2,1,0:T(8,128)(2,1)}, bf16[1,12,128,3072]{3,2,1,0:T(8,128)(2,1)}) fusion(bf16[2,12,128,3072]{3,2,1,0:T(8,128)(2,1)} %param.16), kind=kLoop, calls=%fused_computation.118 | loop fusion | bytes 37748736 | tf_op jit(solution)/shard_map/slice | solution.py:321
  43.8 3.5 convolution_bitcast_fusion.1
  48.9 5.7 %fusion.52 = f32[12,192,128]{2,1,0:T(8,128)S(1)} fusion(bf16[2,3072,12,128]{3,1,2,0:T(8,128)(2,1)} %param.13, bf16[192,3072]{1,0:T(8,128)(2,1)S(1)} %copy-done.5), kind=kOutput, calls=%fused_computation.52 | convolution fusion | flops 1811939328 | bytes 11796480 | tf_op jit(solution)/shard_map/rd,dhe->hre/dot_general | solution.py:314
  55.4 80.2 %attn.2 = bf16[4,4,3,48,128]{4,3,2,1,0:T(8,128)(2,1)S(1)} custom-call(bf16[4,3,192,128]{3,2,1,0:T(8,128)(2,1)S(1)} %pad_maximum_fusion.q_send, bf16[4,2,192,128]{3,2,1,0:T(8,128)(2,1)S(1)} %copy.17.kv_send), custom_call_target="tpu_custom_call" | custom-call | flops 7361003520 | bytes 8388608 | tf_op jit(solution)/shard_map/attn/pallas_call | solution.py:253
  136.5 7.2 %fusion.106 = f32[192,3072]{1,0:T(8,128)} fusion(bf16[192,1536]{1,0:T(8,128)(2,1)S(1)} %reshape.219, bf16[1536,3072]{1,0:T(8,128)(2,1)} %bitcast.119), kind=kOutput, calls=%fused_computation.121 | convolution fusion | flops 1811939328 | bytes 12386304 | tf_op jit(solution)/shard_map/dot_general | solution.py:321
  144.4 14.3 %reduce-scatter.5.cloned.1.call-done = f32[96,3072]{1,0:T(8,128)} async-done(((f32[192,3072]{1,0:T(8,128)}), f32[96,3072]{1,0:T(8,128)}) %reduce-scatter.5.cloned.1.call-update) | async-done | bytes 1179664 | tf_op jit(solution)/shard_map/reduce_scatter | solution.py:322
  162.2 13.2 %all-gather.7.cloned.1.call-done = bf16[192,3072]{1,0:T(8,128)(2,1)} async-done(((bf16[96,3072]{1,0:T(8,128)(2,1)}), bf16[192,3072]{1,0:T(8,128)(2,1)}) %all-gather.7.cloned.1.call-update) | async-done | bytes 1179664 | tf_op jit(solution)/shard_map/all_gather | solution.py:324
  175.4 14.7 %fusion.10 = f32[192,4096]{1,0:T(8,128)} fusion(bf16[192,3072]{1,0:T(8,128)(2,1)} %all-gather.7.cloned.1.call-done, bf16[2,3072,4096]{2,1,0:T(8,128)(2,1)} %param.17), kind=kOutput, calls=%fused_computation.10 | convolution fusion | flops 4831838208 | bytes 29491200 | tf_op jit(solution)/shard_map/dot_general | solution.py:325
  190.1 20.6 %fusion.6 = f32[192,3072]{1,0:T(8,128)} fusion(bf16[2,4096,3072]{2,1,0:T(8,128)(2,1)} %param.19, bf16[192,3072]{1,0:T(8,128)(2,1)S(1)} %copy-done.8, bf16[2,3072,4096]{2,1,0:T(8,128)(2,1)} %param.18, f32[192,4096]{1,0:T(8,128)} %fusion.10), kind=kOutput, calls=%fused_computation.6 | convolution fusion | flops 9668395008 | bytes 57016320 | tf_op jit(solution)/shard_map/dot_general | solution.py:328
  210.9 13.7 %reduce-scatter.7.cloned.1.call-done = f32[96,3072]{1,0:T(8,128)} async-done(((f32[192,3072]{1,0:T(8,128)}), f32[96,3072]{1,0:T(8,128)}) %reduce-scatter.7.cloned.1.call-update) | async-done | bytes 1179664 | tf_op jit(solution)/shard_map/reduce_scatter | solution.py:329
  231.2 3.2 copy.32
  234.4 7.0 %all-gather.9.cloned.1.call-done = bf16[192,3072]{1,0:T(8,128)(2,1)} async-done(((bf16[96,3072]{1,0:T(8,128)(2,1)}), bf16[192,3072]{1,0:T(8,128)(2,1)}) %all-gather.9.cloned.1.call-update) | async-done | bytes 1179664 | tf_op jit(solution)/shard_map/all_gather | solution.py:313
  241.3 3.5 convolution_bitcast_fusion
  245.1 5.7 %fusion.55 = f32[12,192,128]{2,1,0:T(8,128)S(1)} fusion(bf16[2,3072,12,128]{3,1,2,0:T(8,128)(2,1)} %param.13, bf16[192,3072]{1,0:T(8,128)(2,1)S(1)} %copy-done.6), kind=kOutput, calls=%fused_computation.53 | convolution fusion | flops 1811939328 | bytes 11796480 | tf_op jit(solution)/shard_map/rd,dhe->hre/dot_general | solution.py:314
  253.0 78.3 %attn.3 = bf16[4,4,3,48,128]{4,3,2,1,0:T(8,128)(2,1)S(1)} custom-call(bf16[4,3,192,128]{3,2,1,0:T(8,128)(2,1)S(1)} %pad_maximum_fusion.1.q_send, bf16[4,2,192,128]{3,2,1,0:T(8,128)(2,1)S(1)} %pad_maximum_fusion.3.kv_send), custom_call_target="tpu_custom_call" | custom-call | flops 7361003520 | bytes 8388608 | tf_op jit(solution)/shard_map/attn/pallas_call | solution.py:253
  332.2 7.1 %fusion.107 = f32[192,3072]{1,0:T(8,128)} fusion(bf16[192,1536]{1,0:T(8,128)(2,1)S(1)} %reshape.220, bf16[1536,3072]{1,0:T(8,128)(2,1)} %bitcast.118), kind=kOutput, calls=%fused_computation.122 | convolution fusion | flops 1811939328 | bytes 12386304 | tf_op jit(solution)/shard_map/dot_general | solution.py:321
  339.3 14.9 %reduce-scatter.9.cloned.1.call-done = f32[96,3072]{1,0:T(8,128)} async-done(((f32[192,3072]{1,0:T(8,128)}), f32[96,3072]{1,0:T(8,128)}) %reduce-scatter.9.cloned.1.call-update) | async-done | bytes 1179664 | tf_op jit(solution)/shard_map/reduce_scatter | solution.py:322
  357.2 13.0 %all-gather.11.cloned.1.call-done = bf16[192,3072]{1,0:T(8,128)(2,1)} async-done(((bf16[96,3072]{1,0:T(8,128)(2,1)}), bf16[192,3072]{1,0:T(8,128)(2,1)}) %all-gather.11.cloned.1.call-update) | async-done | bytes 1179664 | tf_op jit(solution)/shard_map/all_gather | solution.py:324
  370.1 14.6 %fusion.4 = f32[192,4096]{1,0:T(8,128)} fusion(bf16[192,3072]{1,0:T(8,128)(2,1)} %all-gather.11.cloned.1.call-done, bf16[2,3072,4096]{2,1,0:T(8,128)(2,1)} %param.17), kind=kOutput, calls=%fused_computation.4 | convolution fusion | flops 4831838208 | bytes 29491200 | tf_op jit(solution)/shard_map/dot_general | solution.py:325
  384.7 20.7 %fusion = f32[192,3072]{1,0:T(8,128)} fusion(bf16[2,4096,3072]{2,1,0:T(8,128)(2,1)} %param.19, bf16[192,3072]{1,0:T(8,128)(2,1)S(1)} %copy-done.9, bf16[2,3072,4096]{2,1,0:T(8,128)(2,1)} %param.18, f32[192,4096]{1,0:T(8,128)} %fusion.4), kind=kOutput, calls=%fused_computation | convolution fusion | flops 9668395008 | bytes 57016320 | tf_op jit(solution)/shard_map/dot_general | solution.py:328
  405.4 13.7 %reduce-scatter.11.cloned.1.call-done = f32[96,3072]{1,0:T(8,128)} async-done(((f32[192,3072]{1,0:T(8,128)}), f32[96,3072]{1,0:T(8,128)}) %reduce-scatter.11.cloned.1.call-update) | async-done | bytes 1179664 | tf_op jit(solution)/shard_map/reduce_scatter | solution.py:329
  (76 shorter events, 30.4 us)
Async XLA Ops:
  6.5 37.2 %all-gather.5.cloned.1.call-start = ((), (), s32[]{:S(2)}) async-start(), calls=%async_computation.4 | async-start | bytes 1769472 | tf_op jit(solution)/shard_map/all_gather | solution.py:313
  10.8 148.0 %reduce-scatter.5.cloned.1.call-start = ((), (), s32[]{:S(2)}) async-start(), calls=%async_computation.5 | async-start | bytes 3538944 | tf_op jit(solution)/shard_map/reduce_scatter | solution.py:322
  43.8 3.7 copy-start.5
  143.7 0.7 copy-start.7
  143.7 15.1 %copy-start.4 = (bf16[96,3072]{1,0:T(8,128)(2,1)S(1)}, bf16[96,3072]{1,0:T(8,128)(2,1)}, u32[]{:S(2)}) copy-start(bf16[96,3072]{1,0:T(8,128)(2,1)} %param.10) | copy-start | bytes 1769476
  143.7 31.7 %all-gather.7.cloned.1.call-start = ((), (), s32[]{:S(2)}) async-start(), calls=%async_computation.6 | async-start | bytes 1769472 | tf_op jit(solution)/shard_map/all_gather | solution.py:324
  160.3 0.8 copy-start.3
  162.2 62.4 %reduce-scatter.7.cloned.1.call-start = ((), (), s32[]{:S(2)}) async-start(), calls=%async_computation.7 | async-start | bytes 3538944 | tf_op jit(solution)/shard_map/reduce_scatter | solution.py:329
  175.4 14.7 %copy-start.8 = (bf16[192,3072]{1,0:T(8,128)(2,1)S(1)}, bf16[192,3072]{1,0:T(8,128)(2,1)}, u32[]{:S(2)}) copy-start(bf16[192,3072]{1,0:T(8,128)(2,1)} %all-gather.7.cloned.1.call-done) | copy-start | bytes 3538948
  210.8 17.3 %copy-start = (bf16[1,3072,512]{2,1,0:T(8,128)(2,1)S(1)}, bf16[1,3072,512]{2,1,0:T(8,128)(2,1)}, u32[]{:S(2)}) copy-start(bf16[1,3072,512]{2,1,0:T(8,128)(2,1)} %get-tuple-element.13) | copy-start | bytes 9437188
  210.8 30.5 %all-gather.9.cloned.1.call-start = ((), (), s32[]{:S(2)}) async-start(), calls=%async_computation.8 | async-start | bytes 1769472 | tf_op jit(solution)/shard_map/all_gather | solution.py:313
  226.2 0.8 copy-start.1
  228.1 126.2 %reduce-scatter.9.cloned.1.call-start = ((), (), s32[]{:S(2)}) async-start(), calls=%async_computation.9 | async-start | bytes 3538944 | tf_op jit(solution)/shard_map/reduce_scatter | solution.py:322
  241.3 3.7 copy-start.6
  339.3 15.0 %copy-start.2 = (bf16[96,3072]{1,0:T(8,128)(2,1)S(1)}, bf16[96,3072]{1,0:T(8,128)(2,1)}, u32[]{:S(2)}) copy-start(bf16[96,3072]{1,0:T(8,128)(2,1)} %copy-done.1) | copy-start | bytes 1769476
  339.3 30.9 %all-gather.11.cloned.1.call-start = ((), (), s32[]{:S(2)}) async-start(), calls=%async_computation.10 | async-start | bytes 1769472 | tf_op jit(solution)/shard_map/all_gather | solution.py:324
  356.9 62.2 %reduce-scatter.11.cloned.1.call-start = ((), (), s32[]{:S(2)}) async-start(), calls=%async_computation.11 | async-start | bytes 3538944 | tf_op jit(solution)/shard_map/reduce_scatter | solution.py:329
  370.1 14.6 %copy-start.9 = (bf16[192,3072]{1,0:T(8,128)(2,1)S(1)}, bf16[192,3072]{1,0:T(8,128)(2,1)}, u32[]{:S(2)}) copy-start(bf16[192,3072]{1,0:T(8,128)(2,1)} %all-gather.11.cloned.1.call-done) | copy-start | bytes 3538948
Sparse Core Ops, SparseCore 0:
  10.9 15.4 all-gather.4
  143.8 14.8 reduce-scatter.4
  162.3 13.0 all-gather.6
  210.9 13.5 reduce-scatter.6
  228.2 13.0 all-gather.8
  339.4 14.8 reduce-scatter.8
  357.0 13.0 all-gather.10
  405.5 13.5 reduce-scatter.10

commit v3 on v2

--- a/solution.py
+++ b/solution.py
@@ -6,12 +6,6 @@
 from jax.experimental import pallas as pl
 from jax.experimental.pallas import tpu as pltpu
 from jax.sharding import Mesh, PartitionSpec as P
-
-def rms_norm(hidden, gain):
-    hidden_f = hidden.astype(jnp.float32)
-    inv_rms = lax.rsqrt(jnp.mean(hidden_f * hidden_f, axis=-1, keepdims=True) + 1e-5)
-    return (hidden_f * inv_rms * gain.astype(jnp.float32)).astype(jnp.bfloat16)
-
 
 def seg_positions(dev_ids, rows, dev_total):
     offset = jnp.arange(rows)
@@ -281,6 +275,262 @@
     )(q_send, kv_send)
 
 
+D = 3072
+FF = 4096
+ROWS = 96
+NT = 512
+NO = D // NT
+NG = FF // NT
+NS = 10
+
+
+def dense_kernel(layer, post, qkv, *refs):
+    refs = list(refs)
+    hidden, norms = refs.pop(0), None
+    if post:
+        o_in, nm_mlp, w_o, w_g, w_u, w_d = refs[:6]
+        refs = refs[6:]
+    if qkv:
+        nm_attn, cos_ref, sin_ref, w_q, w_k, w_v = refs[:6]
+        refs = refs[6:]
+    if post:
+        hid_out = refs.pop(0)
+    if qkv:
+        q_out, kv_out = refs[:2]
+        refs = refs[2:]
+    wbuf, wsem = refs[:2]
+    refs = refs[2:]
+    if post:
+        o_mat, hmid, nrm1, act, acc1, snd1, rcv1, acc2, snd2, rcv2, s1, r1, s2, r2 = refs[:14]
+        refs = refs[14:]
+    if qkv:
+        nrm2 = refs.pop(0)
+    sn, rn = refs
+    t_me = lax.axis_index('tp')
+    sibling = {'tp': 1 - t_me}
+
+    n_o = NO if post else 0
+    g0 = n_o
+    d0 = g0 + (2 * NG if post else 0)
+    q0 = d0 + (NO if post else 0)
+    total = q0 + (5 if qkv else 0)
+
+    def cols(i):
+        return pl.ds(pl.multiple_of(i * NT, NT), NT)
+
+    def copies(kind, i, slot):
+        sem = wsem.at[slot]
+        if kind == 'o':
+            return [pltpu.make_async_copy(w_o.at[layer, :, cols(i)], wbuf.at[slot, pl.ds(0, 1536)], sem)]
+        if kind == 'g':
+            return [pltpu.make_async_copy(w_g.at[layer, :, cols(i)], wbuf.at[slot, pl.ds(0, D)], sem)]
+        if kind == 'u':
+            return [pltpu.make_async_copy(w_u.at[layer, :, cols(i)], wbuf.at[slot, pl.ds(0, D)], sem)]
+        if kind == 'd':
+            return [pltpu.make_async_copy(w_d.at[layer, :, cols(i)], wbuf.at[slot], sem)]
+        nl = layer + 1 if post else layer
+        if kind == 'q':
+            return [pltpu.make_async_copy(w_q.at[nl, 4 * i + h], wbuf.at[slot, pl.ds(0, D), pl.ds(h * HD, HD)], sem)
+                    for h in range(4)]
+        if kind == 'k':
+            return [pltpu.make_async_copy(w_k.at[nl], wbuf.at[slot, pl.ds(0, D)], sem)]
+        return [pltpu.make_async_copy(w_v.at[nl], wbuf.at[slot, pl.ds(0, D)], sem)]
+
+    def issue(t):
+        slot = t % NS if isinstance(t, int) else lax.rem(t, NS)
+
+        def go(cond, kind, i):
+            if isinstance(cond, bool):
+                if cond:
+                    for c in copies(kind, i, slot):
+                        c.start()
+            else:
+                @pl.when(cond)
+                def _():
+                    for c in copies(kind, i, slot):
+                        c.start()
+
+        def both(a, b):
+            return (a and b) if isinstance(a, bool) else jnp.logical_and(a, b)
+
+        if post:
+            go(t < n_o, 'o', t)
+            half = (t - g0) // 2
+            even = (t - g0) % 2 == 0
+            inside = both(t >= g0, t < d0)
+            go(both(inside, even), 'g', half)
+            go(both(inside, (t - g0) % 2 == 1), 'u', half)
+            go(both(t >= d0, t < q0), 'd', t - d0)
+        if qkv:
+            go(both(t >= q0, t < q0 + 3), 'q', t - q0)
+            go(t == q0 + 3, 'k', 0)
+            go(t == q0 + 4, 'v', 0)
+
+    def wait(t, depth):
+        slot = t % NS if isinstance(t, int) else lax.rem(t, NS)
+        ref = wbuf.at[slot, pl.ds(0, depth)]
+        pltpu.make_async_copy(ref, ref, wsem.at[slot]).wait()
+        return slot
+
+    barrier = pltpu.get_barrier_semaphore()
+    pl.semaphore_signal(barrier, inc=1, device_id=sibling, device_id_type=pl.DeviceIdType.MESH)
+    for t in range(min(NS, total)):
+        issue(t)
+
+    def send(src, dst, ssem, rsem):
+        return pltpu.make_async_remote_copy(src_ref=src, dst_ref=dst, send_sem=ssem, recv_sem=rsem, device_id=sibling,
+                                            device_id_type=pl.DeviceIdType.MESH)
+
+    def normed(src, gain_row, nrm, idx):
+        ss = jnp.zeros((ROWS, 1), jnp.float32)
+        for j in range(NO):
+            v = src[:, j * NT:(j + 1) * NT].astype(jnp.float32)
+            ss = ss + jnp.sum(v * v, axis=-1, keepdims=True)
+        inv = lax.rsqrt(ss / D + 1e-5)
+        for j in range(NO):
+            sl = slice(j * NT, (j + 1) * NT)
+            nrm[0:ROWS, sl] = (src[:, sl].astype(jnp.float32) * inv * gain_row[:, sl]).astype(jnp.bfloat16)
+        c = send(nrm.at[pl.ds(0, ROWS)], nrm.at[pl.ds(ROWS, ROWS)], sn.at[idx], rn.at[idx])
+        c.start()
+        return c
+
+    def part_copy(snd, rcv, ss, rs, i):
+        return send(snd.at[i], rcv.at[i], ss.at[i], rs.at[i])
+
+    def residual(base, acc, rcv, out, snd, ss, rs):
+        for j in range(NO):
+            part_copy(snd, rcv, ss, rs, j).wait_recv()
+            sl = slice(j * NT, (j + 1) * NT)
+            out[:, sl] = (base[:, sl].astype(jnp.float32) + (acc[j] + rcv[j])).astype(jnp.bfloat16)
+
+    pending = []
+    if post:
+        for blk in range(4):
+            row = pl.multiple_of(jnp.where(t_me == blk // 2, 0, ROWS) + (blk % 2) * SEG, 16)
+            for x in range(XN):
+                for h in range(GRP):
+                    c0 = (x * GRP + h) * HD
+                    o_mat[pl.ds(row, SEG), c0:c0 + HD] = o_in[x, blk, h]
+        pl.semaphore_wait(barrier, 1)
+
+        def o_step(i, carry):
+            slot = wait(i, 1536)
+            p = jnp.dot(o_mat[...], wbuf[slot, pl.ds(0, 1536), :], preferred_element_type=jnp.float32)
+            acc1[i] = p[:ROWS]
+            snd1[i] = p[ROWS:]
+            part_copy(snd1, rcv1, s1, r1, i).start()
+            issue(i + NS)
+            return carry
+
+        lax.fori_loop(0, NO, o_step, 0)
+        residual(hidden, acc1, rcv1, hmid, snd1, s1, r1)
+        c = normed(hmid, nm_mlp[...].astype(jnp.float32)[layer:layer + 1], nrm1, 0)
+        c.wait_recv()
+        pending.append(c)
+
+        def g_step(i, carry):
+            t = g0 + 2 * i
+            slot_g = wait(t, D)
+            g = jnp.dot(nrm1[...], wbuf[slot_g, pl.ds(0, D), :], preferred_element_type=jnp.float32)
+            issue(t + NS)
+            slot_u = wait(t + 1, D)
+            u = jnp.dot(nrm1[...], wbuf[slot_u, pl.ds(0, D), :], preferred_element_type=jnp.float32)
+            act[:, cols(i)] = (g * lax.logistic(g) * u).astype(jnp.bfloat16)
+            issue(t + 1 + NS)
+            return carry
+
+        lax.fori_loop(0, NG, g_step, 0)
+
+        def d_step(i, carry):
+            slot = wait(d0 + i, FF)
+            p = jnp.dot(act[...], wbuf[slot], preferred_element_type=jnp.float32)
+            acc2[i] = p[:ROWS]
+            snd2[i] = p[ROWS:]
+            part_copy(snd2, rcv2, s2, r2, i).start()
+            issue(d0 + i + NS)
+            return carry
+
+        lax.fori_loop(0, NO, d_step, 0)
+        residual(hmid, acc2, rcv2, hid_out, snd2, s2, r2)
+        cur = hid_out
+    else:
+        pl.semaphore_wait(barrier, 1)
+        cur = hidden
+    if qkv:
+        nl = layer + 1 if post else layer
+        c = normed(cur, nm_attn[...].astype(jnp.float32)[nl:nl + 1], nrm2, 1)
+        c.wait_recv()
+        pending.append(c)
+        mine = pl.ds(pl.multiple_of(t_me * ROWS, 16), ROWS)
+        theirs = pl.ds(pl.multiple_of((1 - t_me) * ROWS, 16), ROWS)
+
+        def project(t):
+            slot = wait(t, D)
+            return jnp.dot(nrm2[...], wbuf[slot, pl.ds(0, D), :], preferred_element_type=jnp.float32)
+
+        def rotate(v):
+            return v * cos_ref[...] + pltpu.roll(v, HD // 2, 1) * sin_ref[...]
+
+        def q_step(i, carry):
+            p = project(q0 + i)
+            for h in range(4):
+                r = rotate(p[:, h * HD:(h + 1) * HD]).astype(jnp.bfloat16)
+                q_out[4 * i + h, mine, :] = r[:ROWS]
+                q_out[4 * i + h, theirs, :] = r[ROWS:]
+            return carry
+
+        lax.fori_loop(0, 3, q_step, 0)
+        for which in range(2):
+            p = project(q0 + 3 + which)
+            for h in range(4):
+                r = p[:, h * HD:(h + 1) * HD]
+                r = (rotate(r) if which == 0 else r).astype(jnp.bfloat16)
+                kv_out[h, which, mine, :] = r[:ROWS]
+                kv_out[h, which, theirs, :] = r[ROWS:]
+    for c in pending:
+        c.wait_send()
+    if post:
+        for i in range(NO):
+            part_copy(snd1, rcv1, s1, r1, i).wait_send()
+            part_copy(snd2, rcv2, s2, r2, i).wait_send()
+
+
+def dense(layer, post, qkv, hidden, o=None, norm_mlp=None, w_o=None, w_g=None, w_u=None, w_d=None, norm_attn=None, cos_t=None,
+          sin_t=None, w_q=None, w_k=None, w_v=None):
+    f32, bf16 = jnp.float32, jnp.bfloat16
+    vmem = pl.BlockSpec(memory_space=pltpu.VMEM)
+    hbm = pl.BlockSpec(memory_space=pltpu.HBM)
+    args, specs, outs, scratch = [hidden], [vmem], [], []
+    if post:
+        args += [o, norm_mlp, w_o, w_g, w_u, w_d]
+        specs += [vmem, vmem] + [hbm] * 4
+        outs.append(jax.ShapeDtypeStruct((ROWS, D), bf16))
+    if qkv:
+        args += [norm_attn, cos_t, sin_t, w_q, w_k, w_v]
+        specs += [vmem] * 3 + [hbm] * 3
+        outs += [jax.ShapeDtypeStruct((XN * GRP, TOK, HD), bf16), jax.ShapeDtypeStruct((XN, 2, TOK, HD), bf16)]
+    scratch += [pltpu.VMEM((NS, FF, NT), bf16), pltpu.SemaphoreType.DMA((NS,))]
+    if post:
+        part = pltpu.VMEM((NO, ROWS, NT), f32)
+        scratch += [pltpu.VMEM((TOK, 1536), bf16), pltpu.VMEM((ROWS, D), bf16), pltpu.VMEM((TOK, D), bf16),
+                    pltpu.VMEM((TOK, FF), bf16)] + [part] * 6 + [pltpu.SemaphoreType.DMA((NO,))] * 4
+    if qkv:
+        scratch += [pltpu.VMEM((TOK, D), bf16)]
+    scratch += [pltpu.SemaphoreType.DMA((2,))] * 2
+    moved = (85 << 20 if post else 0) + (16 << 20 if qkv else 0)
+    return pl.pallas_call(
+        functools.partial(dense_kernel, layer, post, qkv),
+        out_shape=tuple(outs),
+        in_specs=specs,
+        out_specs=tuple([vmem] * len(outs)),
+        scratch_shapes=scratch,
+        compiler_params=pltpu.CompilerParams(vmem_limit_bytes=63 << 20, collective_id=2 + layer + (1 if post else 0),
+                                             has_side_effects=True),
+        cost_estimate=pl.CostEstimate(flops=TOK * moved, bytes_accessed=moved, transcendentals=0),
+        name=f'dense{layer}{int(post)}{int(qkv)}',
+    )(*args)
+
+
 def solution(mesh):
     tp_size = mesh.shape['tp']
     cp_size = mesh.shape['cp']
@@ -295,39 +545,26 @@
 
     def body(tokens, norm_attn, norm_mlp, w_q, w_k, w_v, w_o, w_gate, w_up, w_down):
         rows = tokens.shape[0]
-        toks = tp_size * rows
+        tp_idx = lax.axis_index('tp')
         cp_idx = (lax.axis_index('z') * 4 + lax.axis_index('y')) * 4 + lax.axis_index('x')
-        tp_devs = jnp.arange(tp_size) * cp_size + cp_idx
-        pos = seg_positions(tp_devs, rows, dev_total).reshape(toks)
+        tp_devs = jnp.stack([tp_idx, 1 - tp_idx]) * cp_size + cp_idx
+        pos = seg_positions(tp_devs, rows, dev_total).reshape(tp_size * rows)
         inv_freq = 500000.0 ** (-(jnp.arange(HD // 2, dtype=jnp.float32) * 2.0 / HD))
         angles = pos.astype(jnp.float32)[:, None] * inv_freq[None, :]
-        cos_a = jnp.cos(angles)[None]
-        sin_a = jnp.sin(angles)[None]
-
-        def rotary(v):
-            a, b = v[..., :HD // 2], v[..., HD // 2:]
-            return jnp.concatenate([a * cos_a - b * sin_a, b * cos_a + a * sin_a], axis=-1)
-
+        cos_a, sin_a = jnp.cos(angles), jnp.sin(angles)
+        cos_t = jnp.concatenate([cos_a, cos_a], axis=1)
+        sin_t = jnp.concatenate([-sin_a, sin_a], axis=1)
+        layers = w_q.shape[0]
+        proj = dict(norm_attn=norm_attn, cos_t=cos_t, sin_t=sin_t, w_q=w_q.transpose(0, 2, 1, 3), w_k=w_k, w_v=w_v)
+        ffn = dict(norm_mlp=norm_mlp, w_o=w_o.reshape(layers, -1, D), w_g=w_gate, w_u=w_up, w_d=w_down)
         hidden = tokens
-        for layer in range(w_q.shape[0]):
-            normed = lax.all_gather(rms_norm(hidden, norm_attn[layer]), 'tp', axis=0, tiled=True)
-            q_proj = jnp.einsum('rd,dhe->hre', normed, w_q[layer], preferred_element_type=jnp.float32)
-            q_send = rotary(q_proj).astype(jnp.bfloat16).reshape(XN, GRP, toks, HD)
-            k_proj = jnp.einsum('rd,dhe->hre', normed, w_k[layer].reshape(-1, XN, HD), preferred_element_type=jnp.float32)
-            v_proj = jnp.einsum('rd,dhe->hre', normed, w_v[layer].reshape(-1, XN, HD), preferred_element_type=jnp.float32)
-            kv_send = jnp.stack([rotary(k_proj).astype(jnp.bfloat16), v_proj.astype(jnp.bfloat16)], axis=1)
-            o = attention(q_send, kv_send)
-            o = o.transpose(1, 3, 0, 2, 4).reshape(toks, XN * GRP * HD)
-            attn_part = jnp.dot(o, w_o[layer].reshape(XN * GRP * HD, -1), preferred_element_type=jnp.float32)
-            attn_out = lax.psum_scatter(attn_part, 'tp', scatter_dimension=0, tiled=True)
-            hidden_mid = (hidden.astype(jnp.float32) + attn_out).astype(jnp.bfloat16)
-            normed_mlp = lax.all_gather(rms_norm(hidden_mid, norm_mlp[layer]), 'tp', axis=0, tiled=True)
-            gate = jnp.dot(normed_mlp, w_gate[layer], preferred_element_type=jnp.float32)
-            up = jnp.dot(normed_mlp, w_up[layer], preferred_element_type=jnp.float32)
-            act = (jax.nn.silu(gate) * up).astype(jnp.bfloat16)
-            mlp_part = jnp.dot(act, w_down[layer], preferred_element_type=jnp.float32)
-            mlp_out = lax.psum_scatter(mlp_part, 'tp', scatter_dimension=0, tiled=True)
-            hidden = (hidden_mid.astype(jnp.float32) + mlp_out).astype(jnp.bfloat16)
+        q_send, kv_send = dense(0, False, True, hidden, **proj)
+        for layer in range(layers):
+            o = attention(q_send.reshape(XN, GRP, TOK, HD), kv_send)
+            if layer + 1 < layers:
+                hidden, q_send, kv_send = dense(layer, True, True, hidden, o=o, **ffn, **proj)
+            else:
+                hidden, = dense(layer, True, False, hidden, o=o, **ffn)
         return hidden
 
     return jax.shard_map(

time: 429 us -> 251 us (0.59)
  matrix products: 106 us -> 0 us
  waiting for transfers between devices: 89.9 us -> 0 us
  Pallas kernels: 159 us -> 241 us
  local copies, waits for them, and re-layouts: 42.4 us -> 7.73 us
  other arithmetic: 17.1 us -> 1.39 us
  between operations: 13.8 us -> 0.09 us
    dot_general x12 -> x0, matrix products: 106 us -> none  [the longest x2 41.3 us: body(): mlp_part = jnp.dot(act, w_down[layer], preferred_element_type=jnp.float32)]
    pallas_call x0 -> x3, Pallas kernels: none -> 86.8 us  [dense(): pl.pallas_call(functools.partial(dense_kernel, layer, post, qkv), out_sha...]
    reduce_scatter x4 -> x0, waiting for transfers between devices: 56.7 us -> none  [the longest x2 29.3 us: body(): lax.psum_scatter(attn_part, 'tp', scatter_dimension=0, tiled=True)]
    all_gather x4 -> x0, waiting for transfers between devices: 33.1 us -> none  [the longest x2 26.2 us: body(): lax.all_gather(rms_norm(hidden_mid, norm_mlp[layer]), 'tp', axis=0, tiled...]
    slice x3 -> x0, local copies, waits for them, and re-layouts: 26 us -> none  [the longest x1 15.1 us: body(): w_o[layer].reshape(XN * GRP * HD, -1)]
    convert_element_type x5 -> x0, other arithmetic: 7.39 us -> none  [the longest x4 5.19 us: rms_norm(): return (hidden_f * inv_rms * gain.astype(jnp.float32)).astype(jnp.bfloat16)]
    unnamed x24 -> x13, local copies, waits for them, and re-layouts: 14.6 us -> 7.64 us
    reduce_sum x4 -> x0, other arithmetic: 6.06 us -> none  [rms_norm(): jnp.mean(hidden_f * hidden_f, axis=-1, keepdims=True) + 1e-05]
  transfers between devices with their start and end apart: 8 -> 0, of which waited for: 7 -> 0; matrix products, arithmetic and copies ran while one was open for 9% -> 0% of each run, Pallas kernels for 0% -> 0%
where the time goes in v3:
time: 251 us; the launch traced here: 250 us
  Pallas kernels  241 us (96%)
  local copies, waits for them, and re-layouts  7.73 us (3%)
    pallas_call x2, Pallas kernels, attention(): pl.pallas_call(attn_kernel, out_shape=jax.ShapeDtypeStruct((XN, 4, GRP, S...  154 us
    pallas_call x3, Pallas kernels, dense(): pl.pallas_call(functools.partial(dense_kernel, layer, post, qkv), out_sha...  86.8 us
    unnamed x13, local copies, waits for them, and re-layouts  7.64 us

profile of v3, /device:TPU:1, one launch (start us, length us, event | category | flops | bytes accessed | tf_op | source)
XLA Modules:
  0.0 250.4 jit_solution(8967577093384672782)
XLA Ops:
  0.0 0.1 broadcast_subtract_fusion
  0.1 0.1 add_convert_fusion
  0.2 0.1 convert_element_type.11
  0.3 0.4 fusion
  0.7 0.8 pad_maximum_fusion
  1.5 9.8 %dense001.1 = (bf16[12,192,128]{2,1,0:T(8,128)(2,1)}, bf16[4,2,192,128]{3,2,1,0:T(8,128)(2,1)}) custom-call(bf16[96,3072]{1,0:T(8,128)(2,1)} %refs_0_.3, bf16[2,3072]{1,0:T(2,128)(2,1)} %refs_7_.1, f32[192,128]{1,0:T(8,128)} %get-tuple-element.20.refs_2_.refs_8_, f32[192,128]{1,0:T(8,128)} %get-tuple-element.21.refs_3_.refs_9_, ...), custom_call_target="tpu_custom_call" | custom-call | flops 3221225472 | bytes 16777216 | tf_op jit(solution)/shard_map/dense001/pallas_call | solution.py:521
  11.3 0.0 copy-start.3
  11.3 1.1 copy-done.3
  12.4 0.0 copy-start.5
  12.4 1.0 copy-done.5
  13.4 79.3 %attn.2.refs_1_ = bf16[4,4,3,48,128]{4,3,2,1,0:T(8,128)(2,1)S(1)} custom-call(bf16[4,3,192,128]{3,2,1,0:T(8,128)(2,1)S(1)} %bitcast.7, bf16[4,2,192,128]{3,2,1,0:T(8,128)(2,1)S(1)} %copy-done.5), custom_call_target="tpu_custom_call" | custom-call | flops 7361003520 | bytes 8388608 | tf_op jit(solution)/shard_map/attn/pallas_call | solution.py:247
  92.6 0.0 copy-start.1
  92.6 0.8 copy-done.1
  93.5 41.7 %dense011.1 = (bf16[96,3072]{1,0:T(8,128)(2,1)}, bf16[12,192,128]{2,1,0:T(8,128)(2,1)}, bf16[4,2,192,128]{3,2,1,0:T(8,128)(2,1)}) custom-call(bf16[96,3072]{1,0:T(8,128)(2,1)} %refs_0_.3, bf16[4,4,3,48,128]{4,3,2,1,0:T(8,128)(2,1)} %copy-done.1, bf16[2,3072]{1,0:T(2,128)(2,1)} %refs_2_.3, bf16[2,1536,3072]{2,1,0:T(8,128)(2,1)} %bitcast.8, ...), custom_call_target="tpu_custom_call" | custom-call | flops 20333985792 | bytes 105906176 | tf_op jit(solution)/shard_map/dense011/pallas_call | solution.py:521
  135.2 0.0 copy-start.2
  135.2 1.1 copy-done.2
  136.3 0.0 copy-start.4
  136.3 1.0 copy-done.4
  137.2 75.1 %attn.3.refs_1_ = bf16[4,4,3,48,128]{4,3,2,1,0:T(8,128)(2,1)S(1)} custom-call(bf16[4,3,192,128]{3,2,1,0:T(8,128)(2,1)S(1)} %bitcast.6, bf16[4,2,192,128]{3,2,1,0:T(8,128)(2,1)S(1)} %copy-done.4), custom_call_target="tpu_custom_call" | custom-call | flops 7361003520 | bytes 8388608 | tf_op jit(solution)/shard_map/attn/pallas_call | solution.py:247
  212.3 0.0 copy-start
  212.4 0.8 copy-done
  213.2 35.3 %dense110.1 = bf16[96,3072]{1,0:T(8,128)(2,1)} custom-call(bf16[96,3072]{1,0:T(8,128)(2,1)} %get-tuple-element.12.refs_0_, bf16[4,4,3,48,128]{4,3,2,1,0:T(8,128)(2,1)} %copy-done, bf16[2,3072]{1,0:T(2,128)(2,1)} %refs_2_.3, bf16[2,1536,3072]{2,1,0:T(8,128)(2,1)} %bitcast.9, bf16[2,3072,4096]{2,1,0:T(8,128)(2,1)} %refs_4_.3, bf16[2,3072,4096]{2,1,0:T(8,128)(2,1)} %refs_5_.5, ...), custom_call_target="tpu_custom_call" | custom-call | flops 17112760320 | bytes 89128960 | tf_op jit(solution)/shard_map/dense110/pallas_call | solution.py:521
  248.5 1.9 copy.12
  (3 shorter events, 0.0 us)
Async XLA Ops:
  11.3 1.1 copy-start.3
  12.4 1.0 copy-start.5
  92.6 0.8 copy-start.1
  135.2 1.1 copy-start.2
  136.3 1.0 copy-start.4
  212.3 0.8 copy-start

commit v4 on v3

--- a/solution.py
+++ b/solution.py
@@ -26,13 +26,14 @@
 TOK = 192
 SCALE = math.log2(math.e) / math.sqrt(HD)
 NB = 20
+STRIP = 64
 
 
 def quarter_block(quarter):
     return jnp.where(quarter == 0, 0, jnp.where(quarter == 1, 2, jnp.where(quarter == 2, 3, 1)))
 
 
-def attn_kernel(q_send, kv_send, o_out, q_own, kv_all, o_own, o_recv, s_a, s_b, mx_a, mx_b, m_ref, l_ref, acc_ref,
+def attn_kernel(q_send, kv_send, o_out, q_own, kv_all, o_own, o_recv, s_a, s_b, mx_a, mx_b, e_buf, m_ref, l_ref, acc_ref,
                 send_a, recv_a, send_b, recv_b, send_o, recv_o, local_sem):
     zi, yi, xi = lax.axis_index('z'), lax.axis_index('y'), lax.axis_index('x')
     group = zi * 4 + yi
@@ -110,127 +111,159 @@
             stage[half][('b', j, d)].wait_recv()
             begin(half, ('f', j, d), msg(half, 4 + j * 4 + 2 + s, at(a, offs[j], -d), s, b, d))
 
-    for half in range(2):
+    Y, Z = 0, 1
+
+    def send_first(half):
+        for s, d in enumerate((1, -1)):
+            begin(half, ('a', d), msg(half, s, group, None, first[half], d))
+
+    def forward_first(half):
         a = first[half]
         for s, d in enumerate((1, -1)):
-            begin(half, ('a', d), msg(half, s, group, None, a, d))
-    for half in range(2):
-        send_second(half, 0)
-    for half in range(2):
-        a = first[half]
-        for s, d in enumerate((1, -1)):
-            stage[half][('a', d)].wait_recv()
             begin(half, ('g', d), msg(half, 2 + s, at(a, -d, 0), s, a, d))
-    for half in range(2):
-        send_second(half, 1)
-        send_second(half, 2)
-    for half in range(2):
-        forward_second(half, 0)
-    for half in range(2):
+
+    def got(half, *key):
         for d in (1, -1):
-            stage[half][('g', d)].wait_recv()
-        send_second(half, 3)
-    for j in (1, 2, 3):
-        for half in range(2):
-            forward_second(half, j)
+            stage[half][key + (d,)].wait_recv()
+
+    def quarter_rows(t):
+        desc = t >= 2
+        return quarter_block(t), desc, [jnp.where(desc, XN - 1 - i, i) for i in range(XN)]
+
+    def load_q(t):
+        blk, _, xs = quarter_rows(t)
+        row0 = pl.multiple_of(blk * SEG, 16)
+        return jnp.concatenate([q_own[x, h, pl.ds(row0, SEG), :] for h in range(GRP) for x in xs], axis=0)
+
+    def load_kv(kq, zr, which):
+        blk, desc, xs = quarter_rows(kq)
+        krow = pl.multiple_of(blk * SEG, 16)
+        parts = []
+        for r in range(NRUN):
+            member = zr * 4 + jnp.where(desc, NRUN - 1 - r, r)
+            for x in xs:
+                parts.append(kv_all[member, x, which, pl.ds(krow, SEG), :])
+        return jnp.concatenate(parts, axis=0)
+
+    def entry(e, lower, own):
+        n0 = 4 if own else 2
+        u = e - n0
+        t = 1 + jnp.where(u >= 1, 1, 0) + jnp.where(u >= 3, 1, 0)
+        kq = jnp.where(u < 1, 0, jnp.where(u < 3, u - 1, u - 3))
+        t0 = e if own else jnp.where(lower, e, e + 2)
+        return jnp.where(u < 0, t0, t), jnp.where(u < 0, t0, kq)
+
+    def qk(tk, zr, s_ref, mx_ref, own):
+        t, kq = tk
+        s = lax.dot_general(load_q(t), load_kv(kq, zr, 0), (((1,), (1,)), ((), ())), preferred_element_type=jnp.float32)
+        if own:
+            row = lax.broadcasted_iota(jnp.int32, (RUN, CH), 0)
+            col = lax.broadcasted_iota(jnp.int32, (RUN, CH), 1)
+            mine = jnp.where(t >= 2, NRUN - 1 - yi, yi) * RUN
+            visible = col <= row + jnp.where(t == kq, mine, CH)
+            s = jnp.concatenate([jnp.where(visible, s[h * RUN:(h + 1) * RUN], -jnp.inf) for h in range(GRP)], axis=0)
+        s_ref[...] = s
+        mx_ref[...] = jnp.broadcast_to(jnp.max(s, axis=-1, keepdims=True), (QR, HD))
+
+    def soft(tk, zr, s_ref, mx_ref):
+        t, kq = tk
+        vals = load_kv(kq, zr, 1)
+        for h in range(GRP):
+            for r0 in range(h * RUN, (h + 1) * RUN, STRIP):
+                rows = slice(r0, r0 + STRIP)
+                m_old = m_ref[t, rows, :]
+                m_new = jnp.maximum(m_old, mx_ref[rows, :])
+                alpha = jnp.exp2((m_old - m_new) * SCALE)
+                bias = m_new * SCALE
+                lsum = l_ref[t, rows, :] * alpha
+                for c in range(CH // HD):
+                    e = jnp.exp2(s_ref[rows, c * HD:(c + 1) * HD] * SCALE - bias)
+                    lsum = lsum + e
+                    e_buf[rows, c * HD:(c + 1) * HD] = e.astype(jnp.bfloat16)
+                m_ref[t, rows, :] = m_new
+                l_ref[t, rows, :] = lsum
+                acc_ref[t, rows, :] = acc_ref[t, rows, :] * alpha
+            rows = slice(h * RUN, (h + 1) * RUN)
+            acc_ref[t, rows, :] += jnp.dot(e_buf[rows, :], vals, preferred_element_type=jnp.float32)
+
+    def run_row(zr, lower, own, lo, hi, after=None):
+        n = 10 if own else 8
+        if lo == 0:
+            qk(entry(0, lower, own), zr, s_a, mx_a, own)
+
+        def pair(p, carry):
+            qk(entry(2 * p + 1, lower, own), zr, s_b, mx_b, own)
+            soft(entry(2 * p, lower, own), zr, s_a, mx_a)
+            qk(entry(jnp.minimum(2 * p + 2, n - 1), lower, own), zr, s_a, mx_a, own)
+            soft(entry(2 * p + 1, lower, own), zr, s_b, mx_b)
+            if after is not None:
+                after(p)
+            return carry
+
+        lax.fori_loop(lo, hi, pair, 0)
+
+    def o_msg(step, d):
+        to = plus(xi, d)
+        blk = quarter_block(step)
+        return remote(o_own.at[to, blk], o_recv.at[xi, blk], send_o.at[step, d - 1], recv_o.at[step, d - 1], {'x': to})
+
+    def finish(t):
+        blk, _, xs = quarter_rows(t)
+        for h in range(GRP):
+            rows = slice(h * RUN, (h + 1) * RUN)
+            o = (acc_ref[t, rows, :] / jnp.sum(l_ref[t, rows, :], axis=-1, keepdims=True)).astype(jnp.bfloat16)
+            for i in range(XN):
+                o_own[xs[i], blk, h, :, :] = o[i * SEG:(i + 1) * SEG]
+        for d in (2, 1, 3):
+            o_msg(t, d).start()
+
+    send_first(Y)
+    send_second(Y, 0)
+    send_second(Z, 0)
+    send_first(Z)
+    m_ref[...] = jnp.full((4, QR, HD), -jnp.inf, jnp.float32)
+    l_ref[...] = jnp.zeros((4, QR, HD), jnp.float32)
+    acc_ref[...] = jnp.zeros((4, QR, HD), jnp.float32)
+    got(Y, 'a')
+    forward_first(Y)
+    send_second(Y, 1)
+    send_second(Y, 2)
+    forward_second(Z, 0)
+    got(Z, 'a')
+    send_second(Z, 1)
+    send_second(Z, 2)
+    got(Y, 'g')
+    send_second(Y, 3)
+    forward_second(Y, 0)
+    forward_first(Z)
     own_q.wait()
     for c in q_msgs:
         c.wait_recv()
-    for half in range(2):
-        for j in range(4):
-            for d in (1, -1):
-                stage[half][('f', j, d)].wait_recv()
-
-    def flash_quarter(step, carry):
-        quarter = 3 - step
-        blk = quarter_block(quarter)
-        row0 = pl.multiple_of(blk * SEG, 16)
-        desc = quarter >= 2
-        order = quarter * SN + jnp.where(desc, SN - 1 - group, group)
-        last = order // NRUN
-        xs = [jnp.where(desc, XN - 1 - i, i) for i in range(XN)]
-        qs = jnp.concatenate([q_own[x, h, pl.ds(row0, SEG), :] for h in range(GRP) for x in xs], axis=0)
-
-        def load(c, which):
-            kq = c // (SN // NRUN)
-            krow = pl.multiple_of(quarter_block(kq) * SEG, 16)
-            kdesc = kq >= 2
-            parts = []
-            for r in range(NRUN):
-                idx = (c % (SN // NRUN)) * NRUN + r
-                member = jnp.where(kdesc, SN - 1 - idx, idx)
-                for i in range(XN):
-                    x = jnp.where(kdesc, XN - 1 - i, i)
-                    parts.append(kv_all[member, x, which, pl.ds(krow, SEG), :])
-            return jnp.concatenate(parts, axis=0)
-
-        def qk(c, s_ref, mx_ref, masked):
-            s = lax.dot_general(qs, load(c, 0), (((1,), (1,)), ((), ())), preferred_element_type=jnp.float32)
-            if masked:
-                row = lax.broadcasted_iota(jnp.int32, (RUN, CH), 0)
-                col = lax.broadcasted_iota(jnp.int32, (RUN, CH), 1)
-                visible = col <= row + (order - c * NRUN) * RUN
-                s = jnp.concatenate([jnp.where(visible, s[h * RUN:(h + 1) * RUN], -jnp.inf) for h in range(GRP)], axis=0)
-            s_ref[...] = s
-            mx_ref[...] = jnp.broadcast_to(jnp.max(s, axis=-1, keepdims=True), (QR, HD))
-
-        def soft(c, s_ref, mx_ref, valid):
-            vals = load(c, 1)
-            for h in range(GRP):
-                rows = pl.ds(h * RUN, RUN)
-                m_old = m_ref[rows, :]
-                mx = mx_ref[rows, :]
-                if valid is not None:
-                    mx = jnp.where(valid, mx, -jnp.inf)
-                m_new = jnp.maximum(m_old, mx)
-                alpha = jnp.exp2((m_old - m_new) * SCALE)
-                bias = m_new * SCALE
-                if valid is not None:
-                    bias = jnp.where(valid, bias, jnp.inf)
-                lsum = l_ref[rows, :] * alpha
-                es = []
-                for t in range(CH // HD):
-                    e = jnp.exp2(s_ref[rows, t * HD:(t + 1) * HD] * SCALE - bias)
-                    lsum = lsum + e
-                    es.append(e.astype(jnp.bfloat16))
-                pv = jnp.dot(jnp.concatenate(es, axis=1), vals, preferred_element_type=jnp.float32)
-                acc_ref[rows, :] = acc_ref[rows, :] * alpha + pv
-                l_ref[rows, :] = lsum
-                m_ref[rows, :] = m_new
-
-        m_ref[...] = jnp.full((QR, HD), -jnp.inf, jnp.float32)
-        l_ref[...] = jnp.zeros((QR, HD), jnp.float32)
-        acc_ref[...] = jnp.zeros((QR, HD), jnp.float32)
-        qk(last, s_a, mx_a, True)
-
-        def pair(p, carry):
-            c_cur = jnp.where(p == 0, last, 2 * p - 1)
-            c_b = jnp.minimum(2 * p, last)
-            c_a = jnp.minimum(2 * p + 1, last)
-            qk(c_b, s_b, mx_b, False)
-            soft(c_cur, s_a, mx_a, None)
-            qk(c_a, s_a, mx_a, False)
-            soft(c_b, s_b, mx_b, 2 * p < last)
-            return carry
-
-        lax.fori_loop(0, (last + 2) // 2, pair, 0)
-        for h in range(GRP):
-            rows = pl.ds(h * RUN, RUN)
-            o = (acc_ref[rows, :] / jnp.sum(l_ref[rows, :], axis=-1, keepdims=True)).astype(jnp.bfloat16)
-            for i in range(XN):
-                o_own[xs[i], blk, h, :, :] = o[i * SEG:(i + 1) * SEG]
-        for d in (1, 2, 3):
-            to = plus(xi, d)
-            remote(o_own.at[to, blk], o_recv.at[xi, blk], send_o.at[step, d - 1], recv_o.at[step, d - 1], {'x': to}).start()
-        return carry
-
-    lax.fori_loop(0, 4, flash_quarter, 0)
+    got(Z, 'f', 0)
+    rows_z = [plus(zi, d) for d in offs]
+    lower = [r < zi for r in rows_z]
+    run_row(zi, None, True, 0, 3)
+    forward_second(Z, 1)
+    forward_second(Y, 1)
+    run_row(zi, None, True, 3, 5)
+    forward_second(Z, 2)
+    forward_second(Y, 2)
+    got(Z, 'g')
+    send_second(Z, 3)
+    forward_second(Y, 3)
+    got(Z, 'f', 1)
+    run_row(rows_z[1], lower[1], False, 0, 4)
+    forward_second(Z, 3)
+    got(Z, 'f', 2)
+    run_row(rows_z[2], lower[2], False, 0, 4)
+    for j in range(4):
+        got(Y, 'f', j)
+    got(Z, 'f', 3)
+    run_row(rows_z[3], lower[3], False, 0, 4, after=finish)
     o_recv[xi] = o_own[xi]
     for step in range(4):
-        blk = (1, 3, 2, 0)[step]
         for d in (1, 2, 3):
-            to = plus(xi, d)
-            c = remote(o_own.at[to, blk], o_recv.at[xi, blk], send_o.at[step, d - 1], recv_o.at[step, d - 1], {'x': to})
+            c = o_msg(step, d)
             c.wait_send()
             c.wait_recv()
     o_out[...] = o_recv[...]
@@ -258,9 +291,10 @@
             pltpu.VMEM((QR, CH), f32),
             pltpu.VMEM((QR, HD), f32),
             pltpu.VMEM((QR, HD), f32),
-            pltpu.VMEM((QR, HD), f32),
-            pltpu.VMEM((QR, HD), f32),
-            pltpu.VMEM((QR, HD), f32),
+            pltpu.VMEM((QR, CH), bf16),
+            pltpu.VMEM((4, QR, HD), f32),
+            pltpu.VMEM((4, QR, HD), f32),
+            pltpu.VMEM((4, QR, HD), f32),
             pltpu.SemaphoreType.DMA((6,)),
             pltpu.SemaphoreType.DMA((6,)),
             pltpu.SemaphoreType.DMA((2 * NB,)),

time: 251 us -> 226 us (0.900)
  Pallas kernels: 241 us -> 216 us
    pallas_call x2, Pallas kernels: 154 us -> 127 us  [attention(): pl.pallas_call(attn_kernel, out_shape=jax.ShapeDtypeStruct((XN, 4, GRP, S...]
    pallas_call x3, Pallas kernels: 86.8 us -> 89.4 us  [dense(): pl.pallas_call(functools.partial(dense_kernel, layer, post, qkv), out_sha...]
where the time goes in v4:
time: 226 us; the launch traced here: 225 us
  Pallas kernels  216 us (96%)
  local copies, waits for them, and re-layouts  7.73 us (3%)
    pallas_call x2, Pallas kernels, attention(): pl.pallas_call(attn_kernel, out_shape=jax.ShapeDtypeStruct((XN, 4, GRP, S...  127 us
    pallas_call x3, Pallas kernels, dense(): pl.pallas_call(functools.partial(dense_kernel, layer, post, qkv), out_sha...  89.4 us
    unnamed x13, local copies, waits for them, and re-layouts  7.64 us

profile of v4, /device:TPU:1, one launch (start us, length us, event | category | flops | bytes accessed | tf_op | source)
XLA Modules:
  0.0 225.4 jit_solution(3690935637413831498)
XLA Ops:
  0.0 0.1 broadcast_subtract_fusion
  0.1 0.1 add_convert_fusion
  0.2 0.1 convert_element_type.11
  0.3 0.4 fusion
  0.7 0.8 pad_maximum_fusion
  1.5 9.8 %dense001.1 = (bf16[12,192,128]{2,1,0:T(8,128)(2,1)}, bf16[4,2,192,128]{3,2,1,0:T(8,128)(2,1)}) custom-call(bf16[96,3072]{1,0:T(8,128)(2,1)} %refs_0_.3, bf16[2,3072]{1,0:T(2,128)(2,1)} %refs_7_.1, f32[192,128]{1,0:T(8,128)} %get-tuple-element.20.refs_2_.refs_8_, f32[192,128]{1,0:T(8,128)} %get-tuple-element.21.refs_3_.refs_9_, ...), custom_call_target="tpu_custom_call" | custom-call | flops 3221225472 | bytes 16777216 | tf_op jit(solution)/shard_map/dense001/pallas_call | solution.py:555
  11.3 0.0 copy-start.3
  11.3 1.1 copy-done.3
  12.4 0.0 copy-start.5
  12.4 1.0 copy-done.5
  13.4 65.3 %attn.2.refs_1_ = bf16[4,4,3,48,128]{4,3,2,1,0:T(8,128)(2,1)S(1)} custom-call(bf16[4,3,192,128]{3,2,1,0:T(8,128)(2,1)S(1)} %bitcast.7, bf16[4,2,192,128]{3,2,1,0:T(8,128)(2,1)S(1)} %copy-done.5), custom_call_target="tpu_custom_call" | custom-call | flops 7361003520 | bytes 8388608 | tf_op jit(solution)/shard_map/attn/pallas_call | solution.py:280
  78.7 0.0 copy-start.1
  78.7 0.8 copy-done.1
  79.5 41.9 %dense011.1 = (bf16[96,3072]{1,0:T(8,128)(2,1)}, bf16[12,192,128]{2,1,0:T(8,128)(2,1)}, bf16[4,2,192,128]{3,2,1,0:T(8,128)(2,1)}) custom-call(bf16[96,3072]{1,0:T(8,128)(2,1)} %refs_0_.3, bf16[4,4,3,48,128]{4,3,2,1,0:T(8,128)(2,1)} %copy-done.1, bf16[2,3072]{1,0:T(2,128)(2,1)} %refs_2_.3, bf16[2,1536,3072]{2,1,0:T(8,128)(2,1)} %bitcast.8, ...), custom_call_target="tpu_custom_call" | custom-call | flops 20333985792 | bytes 105906176 | tf_op jit(solution)/shard_map/dense011/pallas_call | solution.py:555
  121.4 0.0 copy-start.2
  121.4 1.1 copy-done.2
  122.5 0.0 copy-start.4
  122.5 1.0 copy-done.4
  123.5 61.5 %attn.3.refs_1_ = bf16[4,4,3,48,128]{4,3,2,1,0:T(8,128)(2,1)S(1)} custom-call(bf16[4,3,192,128]{3,2,1,0:T(8,128)(2,1)S(1)} %bitcast.6, bf16[4,2,192,128]{3,2,1,0:T(8,128)(2,1)S(1)} %copy-done.4), custom_call_target="tpu_custom_call" | custom-call | flops 7361003520 | bytes 8388608 | tf_op jit(solution)/shard_map/attn/pallas_call | solution.py:280
  185.0 0.0 copy-start
  185.0 0.8 copy-done
  185.8 37.7 %dense110.1 = bf16[96,3072]{1,0:T(8,128)(2,1)} custom-call(bf16[96,3072]{1,0:T(8,128)(2,1)} %get-tuple-element.12.refs_0_, bf16[4,4,3,48,128]{4,3,2,1,0:T(8,128)(2,1)} %copy-done, bf16[2,3072]{1,0:T(2,128)(2,1)} %refs_2_.3, bf16[2,1536,3072]{2,1,0:T(8,128)(2,1)} %bitcast.9, bf16[2,3072,4096]{2,1,0:T(8,128)(2,1)} %refs_4_.3, bf16[2,3072,4096]{2,1,0:T(8,128)(2,1)} %refs_5_.5, ...), custom_call_target="tpu_custom_call" | custom-call | flops 17112760320 | bytes 89128960 | tf_op jit(solution)/shard_map/dense110/pallas_call | solution.py:555
  223.5 1.9 copy.12
  (3 shorter events, 0.0 us)
Async XLA Ops:
  11.3 1.1 copy-start.3
  12.4 1.0 copy-start.5
  78.7 0.8 copy-start.1
  121.4 1.1 copy-start.2
  122.5 1.0 copy-start.4
  185.0 0.8 copy-start

commit v5 on v4

--- a/solution.py
+++ b/solution.py
@@ -25,7 +25,7 @@
 QR = GRP * RUN
 TOK = 192
 SCALE = math.log2(math.e) / math.sqrt(HD)
-NB = 20
+NB = 24
 STRIP = 64
 
 
@@ -33,8 +33,8 @@
     return jnp.where(quarter == 0, 0, jnp.where(quarter == 1, 2, jnp.where(quarter == 2, 3, 1)))
 
 
-def attn_kernel(q_send, kv_send, o_out, q_own, kv_all, o_own, o_recv, s_a, s_b, mx_a, mx_b, e_buf, m_ref, l_ref, acc_ref,
-                send_a, recv_a, send_b, recv_b, send_o, recv_o, local_sem):
+def attn_kernel(q_send, kv_send, o_out, q_own, kv_all, o_own, o_recv, s_a, s_b, e_buf, m_ref, l_ref, acc_ref,
+                send_a, recv_a, send_b, recv_b, send_o, recv_o):
     zi, yi, xi = lax.axis_index('z'), lax.axis_index('y'), lax.axis_index('x')
     group = zi * 4 + yi
 
@@ -50,28 +50,20 @@
     for d in (1, -1):
         pl.semaphore_signal(barrier, inc=1, device_id={'y': plus(yi, d)}, device_id_type=pl.DeviceIdType.MESH)
         pl.semaphore_signal(barrier, inc=1, device_id={'z': plus(zi, d)}, device_id_type=pl.DeviceIdType.MESH)
-    own_q = pltpu.make_async_copy(q_send.at[xi], q_own.at[xi], local_sem.at[0])
-    own_kv = pltpu.make_async_copy(kv_send.at[xi], kv_all.at[group, xi], local_sem.at[1])
-    own_q.start()
-    own_kv.start()
     pl.semaphore_wait(barrier, 7)
 
     def remote(src, dst, ssem, rsem, dev):
         return pltpu.make_async_remote_copy(src_ref=src, dst_ref=dst, send_sem=ssem, recv_sem=rsem, device_id=dev,
                                             device_id_type=pl.DeviceIdType.MESH)
 
-    kv_msgs, q_msgs = [], []
-    for d in (1, 2, 3):
+    kv_msgs, q_msgs = {}, {}
+    for d in (1, 3, 2):
         to = plus(xi, d)
-        kv_msgs.append(remote(kv_send.at[to], kv_all.at[group, xi], send_a.at[d - 1], recv_a.at[d - 1], {'x': to}))
-        q_msgs.append(remote(q_send.at[to], q_own.at[xi], send_a.at[d + 2], recv_a.at[d + 2], {'x': to}))
-    for c in kv_msgs:
-        c.start()
-    for c in q_msgs:
-        c.start()
-    own_kv.wait()
-    for c in kv_msgs:
-        c.wait_recv()
+        kv_msgs[d] = remote(kv_send.at[to], kv_all.at[group, 4 - d], send_a.at[d - 1], recv_a.at[d - 1], {'x': to})
+        kv_msgs[d].start()
+    for d in (1, 3, 2):
+        to = plus(xi, d)
+        q_msgs[d] = remote(q_send.at[to], q_own.at[xi], send_a.at[d + 2], recv_a.at[d + 2], {'x': to})
 
     pos = (zi, yi)
     names = ('z', 'y')
@@ -98,29 +90,42 @@
         stage[half][key] = m
         m.start()
 
+    def send_own(part):
+        half, p = part // 2, part % 2
+        a = first[half]
+        src = kv_send.at[xi] if part == 0 else kv_all.at[group, part]
+        for s, d in enumerate((1, -1)):
+            for key, base, axis in (('a', 0, a), ('b0', 6, 1 - a)):
+                k = half * NB + base + p * 2 + s
+                begin(half, (key, p, d), remote(src, kv_all.at[group, part], send_b.at[k], recv_b.at[k],
+                                                {names[axis]: plus(pos[axis], d)}))
+
     def send_second(half, j):
         a = first[half]
         b = 1 - a
         for s, d in enumerate((1, -1)):
-            begin(half, ('b', j, d), msg(half, 4 + j * 4 + s, at(a, offs[j], 0), None, b, d))
+            begin(half, ('b', j, d), msg(half, 8 + j * 4 + s, at(a, offs[j], 0), None, b, d))
 
     def forward_second(half, j):
         a = first[half]
         b = 1 - a
         for s, d in enumerate((1, -1)):
-            stage[half][('b', j, d)].wait_recv()
-            begin(half, ('f', j, d), msg(half, 4 + j * 4 + 2 + s, at(a, offs[j], -d), s, b, d))
+            stage[half][('b0', s, d) if j == 0 else ('b', j, d)].wait_recv()
+            k = 10 + s if j == 0 else 10 + j * 4 + s
+            begin(half, ('f', j, d), msg(half, k, at(a, offs[j], -d), s, b, d))
+        if j == 0:
+            for s, d in enumerate((1, -1)):
+                stage[half][('b0', 1 - s, d)].wait_recv()
 
     Y, Z = 0, 1
-
-    def send_first(half):
-        for s, d in enumerate((1, -1)):
-            begin(half, ('a', d), msg(half, s, group, None, first[half], d))
 
     def forward_first(half):
         a = first[half]
         for s, d in enumerate((1, -1)):
-            begin(half, ('g', d), msg(half, 2 + s, at(a, -d, 0), s, a, d))
+            stage[half][('a', s, d)].wait_recv()
+            begin(half, ('g', d), msg(half, 4 + s, at(a, -d, 0), s, a, d))
+        for s, d in enumerate((1, -1)):
+            stage[half][('a', 1 - s, d)].wait_recv()
 
     def got(half, *key):
         for d in (1, -1):
@@ -142,7 +147,7 @@
         for r in range(NRUN):
             member = zr * 4 + jnp.where(desc, NRUN - 1 - r, r)
             for x in xs:
-                parts.append(kv_all[member, x, which, pl.ds(krow, SEG), :])
+                parts.append(kv_all[member, plus(x, -xi), which, pl.ds(krow, SEG), :])
         return jnp.concatenate(parts, axis=0)
 
     def entry(e, lower, own):
@@ -153,7 +158,7 @@
         t0 = e if own else jnp.where(lower, e, e + 2)
         return jnp.where(u < 0, t0, t), jnp.where(u < 0, t0, kq)
 
-    def qk(tk, zr, s_ref, mx_ref, own):
+    def qk(tk, zr, s_ref, own):
         t, kq = tk
         s = lax.dot_general(load_q(t), load_kv(kq, zr, 0), (((1,), (1,)), ((), ())), preferred_element_type=jnp.float32)
         if own:
@@ -163,16 +168,18 @@
             visible = col <= row + jnp.where(t == kq, mine, CH)
             s = jnp.concatenate([jnp.where(visible, s[h * RUN:(h + 1) * RUN], -jnp.inf) for h in range(GRP)], axis=0)
         s_ref[...] = s
-        mx_ref[...] = jnp.broadcast_to(jnp.max(s, axis=-1, keepdims=True), (QR, HD))
-
-    def soft(tk, zr, s_ref, mx_ref):
+
+    def soft(tk, zr, s_ref):
         t, kq = tk
         vals = load_kv(kq, zr, 1)
         for h in range(GRP):
             for r0 in range(h * RUN, (h + 1) * RUN, STRIP):
                 rows = slice(r0, r0 + STRIP)
                 m_old = m_ref[t, rows, :]
-                m_new = jnp.maximum(m_old, mx_ref[rows, :])
+                mx = s_ref[rows, 0:HD]
+                for c in range(1, CH // HD):
+                    mx = jnp.maximum(mx, s_ref[rows, c * HD:(c + 1) * HD])
+                m_new = jnp.maximum(m_old, jnp.max(mx, axis=-1, keepdims=True))
                 alpha = jnp.exp2((m_old - m_new) * SCALE)
                 bias = m_new * SCALE
                 lsum = l_ref[t, rows, :] * alpha
@@ -189,13 +196,13 @@
     def run_row(zr, lower, own, lo, hi, after=None):
         n = 10 if own else 8
         if lo == 0:
-            qk(entry(0, lower, own), zr, s_a, mx_a, own)
+            qk(entry(0, lower, own), zr, s_a, own)
 
         def pair(p, carry):
-            qk(entry(2 * p + 1, lower, own), zr, s_b, mx_b, own)
-            soft(entry(2 * p, lower, own), zr, s_a, mx_a)
-            qk(entry(jnp.minimum(2 * p + 2, n - 1), lower, own), zr, s_a, mx_a, own)
-            soft(entry(2 * p + 1, lower, own), zr, s_b, mx_b)
+            qk(entry(2 * p + 1, lower, own), zr, s_b, own)
+            soft(entry(2 * p, lower, own), zr, s_a)
+            qk(entry(jnp.minimum(2 * p + 2, n - 1), lower, own), zr, s_a, own)
+            soft(entry(2 * p + 1, lower, own), zr, s_b)
             if after is not None:
                 after(p)
             return carry
@@ -217,27 +224,31 @@
         for d in (2, 1, 3):
             o_msg(t, d).start()
 
-    send_first(Y)
-    send_second(Y, 0)
-    send_second(Z, 0)
-    send_first(Z)
+    send_own(0)
+    for d in (1, 3, 2):
+        q_msgs[d].start()
+    kv_all[group, 0] = kv_send[xi]
+    q_own[xi] = q_send[xi]
+    kv_msgs[3].wait_recv()
+    send_own(1)
+    kv_msgs[1].wait_recv()
+    send_own(3)
+    kv_msgs[2].wait_recv()
+    send_own(2)
     m_ref[...] = jnp.full((4, QR, HD), -jnp.inf, jnp.float32)
     l_ref[...] = jnp.zeros((4, QR, HD), jnp.float32)
     acc_ref[...] = jnp.zeros((4, QR, HD), jnp.float32)
-    got(Y, 'a')
     forward_first(Y)
     send_second(Y, 1)
     send_second(Y, 2)
     forward_second(Z, 0)
-    got(Z, 'a')
+    forward_first(Z)
     send_second(Z, 1)
     send_second(Z, 2)
     got(Y, 'g')
     send_second(Y, 3)
     forward_second(Y, 0)
-    forward_first(Z)
-    own_q.wait()
-    for c in q_msgs:
+    for c in q_msgs.values():
         c.wait_recv()
     got(Z, 'f', 0)
     rows_z = [plus(zi, d) for d in offs]
@@ -267,7 +278,7 @@
             c.wait_send()
             c.wait_recv()
     o_out[...] = o_recv[...]
-    for c in kv_msgs + q_msgs:
+    for c in list(kv_msgs.values()) + list(q_msgs.values()):
         c.wait_send()
     for half in range(2):
         for c in stage[half].values():
@@ -280,7 +291,7 @@
     return pl.pallas_call(
         attn_kernel,
         out_shape=jax.ShapeDtypeStruct((XN, 4, GRP, SEG, HD), bf16),
-        in_specs=[pl.BlockSpec(memory_space=pltpu.HBM)] * 2,
+        in_specs=[pl.BlockSpec(memory_space=pltpu.VMEM)] * 2,
         out_specs=pl.BlockSpec(memory_space=pltpu.VMEM),
         scratch_shapes=[
             pltpu.VMEM((XN, GRP, TOK, HD), bf16),
@@ -289,8 +300,6 @@
             pltpu.VMEM((XN, 4, GRP, SEG, HD), bf16),
             pltpu.VMEM((QR, CH), f32),
             pltpu.VMEM((QR, CH), f32),
-            pltpu.VMEM((QR, HD), f32),
-            pltpu.VMEM((QR, HD), f32),
             pltpu.VMEM((QR, CH), bf16),
             pltpu.VMEM((4, QR, HD), f32),
             pltpu.VMEM((4, QR, HD), f32),
@@ -301,7 +310,6 @@
             pltpu.SemaphoreType.DMA((2 * NB,)),
             pltpu.SemaphoreType.DMA((4, 3)),
             pltpu.SemaphoreType.DMA((4, 3)),
-            pltpu.SemaphoreType.DMA((2,)),
         ],
         compiler_params=pltpu.CompilerParams(vmem_limit_bytes=40 << 20, collective_id=1, has_side_effects=True),
         cost_estimate=pl.CostEstimate(flops=2 * 2 * 130 * 192 * 576 * 128, bytes_accessed=8 << 20, transcendentals=0),

time: 226 us -> 210 us (0.929)
  Pallas kernels: 216 us -> 200 us
    pallas_call x2, Pallas kernels: 127 us -> 109 us  [attention(): pl.pallas_call(attn_kernel, out_shape=jax.ShapeDtypeStruct((XN, 4, GRP, S...]
where the time goes in v5:
time: 210 us; the launch traced here: 209 us
  Pallas kernels  200 us (95%)
  local copies, waits for them, and re-layouts  7.73 us (4%)
    pallas_call x2, Pallas kernels, attention(): pl.pallas_call(attn_kernel, out_shape=jax.ShapeDtypeStruct((XN, 4, GRP, S...  109 us
    pallas_call x3, Pallas kernels, dense(): pl.pallas_call(functools.partial(dense_kernel, layer, post, qkv), out_sha...  91 us
    unnamed x13, local copies, waits for them, and re-layouts  7.64 us

profile of v5, /device:TPU:1, one launch (start us, length us, event | category | flops | bytes accessed | tf_op | source)
XLA Modules:
  0.0 209.5 jit_solution(10388562903400700638)
XLA Ops:
  0.0 0.1 broadcast_subtract_fusion
  0.1 0.1 add_convert_fusion
  0.2 0.1 convert_element_type.11
  0.3 0.4 fusion
  0.7 0.8 pad_maximum_fusion
  1.5 9.8 %dense001.1 = (bf16[12,192,128]{2,1,0:T(8,128)(2,1)}, bf16[4,2,192,128]{3,2,1,0:T(8,128)(2,1)}) custom-call(bf16[96,3072]{1,0:T(8,128)(2,1)} %refs_0_.3, bf16[2,3072]{1,0:T(2,128)(2,1)} %refs_7_.1, f32[192,128]{1,0:T(8,128)} %get-tuple-element.20.refs_2_.refs_8_, f32[192,128]{1,0:T(8,128)} %get-tuple-element.21.refs_3_.refs_9_, ...), custom_call_target="tpu_custom_call" | custom-call | flops 3221225472 | bytes 16777216 | tf_op jit(solution)/shard_map/dense001/pallas_call | solution.py:563
  11.3 0.0 copy-start.3
  11.3 1.1 copy-done.3
  12.4 0.0 copy-start.5
  12.4 1.0 copy-done.5
  13.4 56.7 %attn.2.refs_1_ = bf16[4,4,3,48,128]{4,3,2,1,0:T(8,128)(2,1)S(1)} custom-call(bf16[4,3,192,128]{3,2,1,0:T(8,128)(2,1)S(1)} %bitcast.7, bf16[4,2,192,128]{3,2,1,0:T(8,128)(2,1)S(1)} %copy-done.5), custom_call_target="tpu_custom_call" | custom-call | flops 7361003520 | bytes 8388608 | tf_op jit(solution)/shard_map/attn/pallas_call | solution.py:291
  70.1 0.0 copy-start.1
  70.1 0.8 copy-done.1
  70.9 43.5 %dense011.1 = (bf16[96,3072]{1,0:T(8,128)(2,1)}, bf16[12,192,128]{2,1,0:T(8,128)(2,1)}, bf16[4,2,192,128]{3,2,1,0:T(8,128)(2,1)}) custom-call(bf16[96,3072]{1,0:T(8,128)(2,1)} %refs_0_.3, bf16[4,4,3,48,128]{4,3,2,1,0:T(8,128)(2,1)} %copy-done.1, bf16[2,3072]{1,0:T(2,128)(2,1)} %refs_2_.3, bf16[2,1536,3072]{2,1,0:T(8,128)(2,1)} %bitcast.8, ...), custom_call_target="tpu_custom_call" | custom-call | flops 20333985792 | bytes 105906176 | tf_op jit(solution)/shard_map/dense011/pallas_call | solution.py:563
  114.4 0.0 copy-start.2
  114.4 1.1 copy-done.2
  115.4 0.0 copy-start.4
  115.4 1.0 copy-done.4
  116.4 52.5 %attn.3.refs_1_ = bf16[4,4,3,48,128]{4,3,2,1,0:T(8,128)(2,1)S(1)} custom-call(bf16[4,3,192,128]{3,2,1,0:T(8,128)(2,1)S(1)} %bitcast.6, bf16[4,2,192,128]{3,2,1,0:T(8,128)(2,1)S(1)} %copy-done.4), custom_call_target="tpu_custom_call" | custom-call | flops 7361003520 | bytes 8388608 | tf_op jit(solution)/shard_map/attn/pallas_call | solution.py:291
  169.0 0.0 copy-start
  169.0 0.8 copy-done
  169.8 37.8 %dense110.1 = bf16[96,3072]{1,0:T(8,128)(2,1)} custom-call(bf16[96,3072]{1,0:T(8,128)(2,1)} %get-tuple-element.12.refs_0_, bf16[4,4,3,48,128]{4,3,2,1,0:T(8,128)(2,1)} %copy-done, bf16[2,3072]{1,0:T(2,128)(2,1)} %refs_2_.3, bf16[2,1536,3072]{2,1,0:T(8,128)(2,1)} %bitcast.9, bf16[2,3072,4096]{2,1,0:T(8,128)(2,1)} %refs_4_.3, bf16[2,3072,4096]{2,1,0:T(8,128)(2,1)} %refs_5_.5, ...), custom_call_target="tpu_custom_call" | custom-call | flops 17112760320 | bytes 89128960 | tf_op jit(solution)/shard_map/dense110/pallas_call | solution.py:563
  207.6 1.9 copy.12
  (3 shorter events, 0.0 us)
Async XLA Ops:
  11.3 1.1 copy-start.3
  12.4 1.0 copy-start.5
  70.1 0.8 copy-start.1
  114.4 1.1 copy-start.2
  115.4 1.0 copy-start.4
  169.0 0.8 copy-start

commit v6 on v5

--- a/solution.py
+++ b/solution.py
@@ -33,7 +33,7 @@
     return jnp.where(quarter == 0, 0, jnp.where(quarter == 1, 2, jnp.where(quarter == 2, 3, 1)))
 
 
-def attn_kernel(q_send, kv_send, o_out, q_own, kv_all, o_own, o_recv, s_a, s_b, e_buf, m_ref, l_ref, acc_ref,
+def attend(fill, q_send, kv_send, q_own, kv_all, o_own, o_recv, s_a, s_b, e_buf, m_ref, l_ref, acc_ref,
                 send_a, recv_a, send_b, recv_b, send_o, recv_o):
     zi, yi, xi = lax.axis_index('z'), lax.axis_index('y'), lax.axis_index('x')
     group = zi * 4 + yi
@@ -50,7 +50,9 @@
     for d in (1, -1):
         pl.semaphore_signal(barrier, inc=1, device_id={'y': plus(yi, d)}, device_id_type=pl.DeviceIdType.MESH)
         pl.semaphore_signal(barrier, inc=1, device_id={'z': plus(zi, d)}, device_id_type=pl.DeviceIdType.MESH)
-    pl.semaphore_wait(barrier, 7)
+    pl.semaphore_signal(barrier, inc=1, device_id={'tp': 1 - lax.axis_index('tp')}, device_id_type=pl.DeviceIdType.MESH)
+    fill()
+    pl.semaphore_wait(barrier, 8)
 
     def remote(src, dst, ssem, rsem, dev):
         return pltpu.make_async_remote_copy(src_ref=src, dst_ref=dst, send_sem=ssem, recv_sem=rsem, device_id=dev,
@@ -277,7 +279,6 @@
             c = o_msg(step, d)
             c.wait_send()
             c.wait_recv()
-    o_out[...] = o_recv[...]
     for c in list(kv_msgs.values()) + list(q_msgs.values()):
         c.wait_send()
     for half in range(2):
@@ -285,36 +286,27 @@
             c.wait_send()
 
 
-def attention(q_send, kv_send):
+def attn_scratch():
     f32 = jnp.float32
     bf16 = jnp.bfloat16
-    return pl.pallas_call(
-        attn_kernel,
-        out_shape=jax.ShapeDtypeStruct((XN, 4, GRP, SEG, HD), bf16),
-        in_specs=[pl.BlockSpec(memory_space=pltpu.VMEM)] * 2,
-        out_specs=pl.BlockSpec(memory_space=pltpu.VMEM),
-        scratch_shapes=[
-            pltpu.VMEM((XN, GRP, TOK, HD), bf16),
-            pltpu.VMEM((SN, XN, 2, TOK, HD), bf16),
-            pltpu.VMEM((XN, 4, GRP, SEG, HD), bf16),
-            pltpu.VMEM((XN, 4, GRP, SEG, HD), bf16),
-            pltpu.VMEM((QR, CH), f32),
-            pltpu.VMEM((QR, CH), f32),
-            pltpu.VMEM((QR, CH), bf16),
-            pltpu.VMEM((4, QR, HD), f32),
-            pltpu.VMEM((4, QR, HD), f32),
-            pltpu.VMEM((4, QR, HD), f32),
-            pltpu.SemaphoreType.DMA((6,)),
-            pltpu.SemaphoreType.DMA((6,)),
-            pltpu.SemaphoreType.DMA((2 * NB,)),
-            pltpu.SemaphoreType.DMA((2 * NB,)),
-            pltpu.SemaphoreType.DMA((4, 3)),
-            pltpu.SemaphoreType.DMA((4, 3)),
-        ],
-        compiler_params=pltpu.CompilerParams(vmem_limit_bytes=40 << 20, collective_id=1, has_side_effects=True),
-        cost_estimate=pl.CostEstimate(flops=2 * 2 * 130 * 192 * 576 * 128, bytes_accessed=8 << 20, transcendentals=0),
-        name='attn',
-    )(q_send, kv_send)
+    return [
+        pltpu.VMEM((XN, GRP, TOK, HD), bf16),
+        pltpu.VMEM((SN, XN, 2, TOK, HD), bf16),
+        pltpu.VMEM((XN, 4, GRP, SEG, HD), bf16),
+        pltpu.VMEM((XN, 4, GRP, SEG, HD), bf16),
+        pltpu.VMEM((QR, CH), f32),
+        pltpu.VMEM((QR, CH), f32),
+        pltpu.VMEM((QR, CH), bf16),
+        pltpu.VMEM((4, QR, HD), f32),
+        pltpu.VMEM((4, QR, HD), f32),
+        pltpu.VMEM((4, QR, HD), f32),
+        pltpu.SemaphoreType.DMA((6,)),
+        pltpu.SemaphoreType.DMA((6,)),
+        pltpu.SemaphoreType.DMA((2 * NB,)),
+        pltpu.SemaphoreType.DMA((2 * NB,)),
+        pltpu.SemaphoreType.DMA((4, 3)),
+        pltpu.SemaphoreType.DMA((4, 3)),
+    ]
 
 
 D = 3072
@@ -323,15 +315,15 @@
 NT = 512
 NO = D // NT
 NG = FF // NT
-NS = 10
+NS = 7
 
 
 def dense_kernel(layer, post, qkv, *refs):
     refs = list(refs)
     hidden, norms = refs.pop(0), None
     if post:
-        o_in, nm_mlp, w_o, w_g, w_u, w_d = refs[:6]
-        refs = refs[6:]
+        q_send, kv_send, nm_mlp, w_o, w_g, w_u, w_d = refs[:7]
+        refs = refs[7:]
     if qkv:
         nm_attn, cos_ref, sin_ref, w_q, w_k, w_v = refs[:6]
         refs = refs[6:]
@@ -343,6 +335,8 @@
     wbuf, wsem = refs[:2]
     refs = refs[2:]
     if post:
+        attn_refs, refs = refs[:16], refs[16:]
+        o_in = attn_refs[3]
         o_mat, hmid, nrm1, act, acc1, snd1, rcv1, acc2, snd2, rcv2, s1, r1, s2, r2 = refs[:14]
         refs = refs[14:]
     if qkv:
@@ -351,7 +345,7 @@
     t_me = lax.axis_index('tp')
     sibling = {'tp': 1 - t_me}
 
-    n_o = NO if post else 0
+    n_o = NO // 2 if post else 0
     g0 = n_o
     d0 = g0 + (2 * NG if post else 0)
     q0 = d0 + (NO if post else 0)
@@ -363,7 +357,8 @@
     def copies(kind, i, slot):
         sem = wsem.at[slot]
         if kind == 'o':
-            return [pltpu.make_async_copy(w_o.at[layer, :, cols(i)], wbuf.at[slot, pl.ds(0, 1536)], sem)]
+            return [pltpu.make_async_copy(w_o.at[layer, :, cols(2 * i + p)], wbuf.at[slot, pl.ds(p * 1536, 1536)], sem)
+                    for p in range(2)]
         if kind == 'g':
             return [pltpu.make_async_copy(w_g.at[layer, :, cols(i)], wbuf.at[slot, pl.ds(0, D)], sem)]
         if kind == 'u':
@@ -414,10 +409,16 @@
         pltpu.make_async_copy(ref, ref, wsem.at[slot]).wait()
         return slot
 
-    barrier = pltpu.get_barrier_semaphore()
-    pl.semaphore_signal(barrier, inc=1, device_id=sibling, device_id_type=pl.DeviceIdType.MESH)
-    for t in range(min(NS, total)):
-        issue(t)
+    def fill():
+        for t in range(min(NS, total)):
+            issue(t)
+
+    if post:
+        attend(fill, q_send, kv_send, *attn_refs)
+    else:
+        barrier = pltpu.get_barrier_semaphore()
+        pl.semaphore_signal(barrier, inc=1, device_id=sibling, device_id_type=pl.DeviceIdType.MESH)
+        fill()
 
     def send(src, dst, ssem, rsem):
         return pltpu.make_async_remote_copy(src_ref=src, dst_ref=dst, send_sem=ssem, recv_sem=rsem, device_id=sibling,
@@ -453,18 +454,18 @@
                 for h in range(GRP):
                     c0 = (x * GRP + h) * HD
                     o_mat[pl.ds(row, SEG), c0:c0 + HD] = o_in[x, blk, h]
-        pl.semaphore_wait(barrier, 1)
 
         def o_step(i, carry):
-            slot = wait(i, 1536)
-            p = jnp.dot(o_mat[...], wbuf[slot, pl.ds(0, 1536), :], preferred_element_type=jnp.float32)
-            acc1[i] = p[:ROWS]
-            snd1[i] = p[ROWS:]
-            part_copy(snd1, rcv1, s1, r1, i).start()
+            slot = wait(i, D)
+            for q in range(2):
+                p = jnp.dot(o_mat[...], wbuf[slot, pl.ds(q * 1536, 1536), :], preferred_element_type=jnp.float32)
+                acc1[2 * i + q] = p[:ROWS]
+                snd1[2 * i + q] = p[ROWS:]
+                part_copy(snd1, rcv1, s1, r1, 2 * i + q).start()
             issue(i + NS)
             return carry
 
-        lax.fori_loop(0, NO, o_step, 0)
+        lax.fori_loop(0, NO // 2, o_step, 0)
         residual(hidden, acc1, rcv1, hmid, snd1, s1, r1)
         c = normed(hmid, nm_mlp[...].astype(jnp.float32)[layer:layer + 1], nrm1, 0)
         c.wait_recv()
@@ -537,15 +538,15 @@
             part_copy(snd2, rcv2, s2, r2, i).wait_send()
 
 
-def dense(layer, post, qkv, hidden, o=None, norm_mlp=None, w_o=None, w_g=None, w_u=None, w_d=None, norm_attn=None, cos_t=None,
+def dense(layer, post, qkv, hidden, q_send=None, kv_send=None, norm_mlp=None, w_o=None, w_g=None, w_u=None, w_d=None, norm_attn=None, cos_t=None,
           sin_t=None, w_q=None, w_k=None, w_v=None):
     f32, bf16 = jnp.float32, jnp.bfloat16
     vmem = pl.BlockSpec(memory_space=pltpu.VMEM)
     hbm = pl.BlockSpec(memory_space=pltpu.HBM)
     args, specs, outs, scratch = [hidden], [vmem], [], []
     if post:
-        args += [o, norm_mlp, w_o, w_g, w_u, w_d]
-        specs += [vmem, vmem] + [hbm] * 4
+        args += [q_send, kv_send, norm_mlp, w_o, w_g, w_u, w_d]
+        specs += [vmem] * 3 + [hbm] * 4
         outs.append(jax.ShapeDtypeStruct((ROWS, D), bf16))
     if qkv:
         args += [norm_attn, cos_t, sin_t, w_q, w_k, w_v]
@@ -554,7 +555,7 @@
     scratch += [pltpu.VMEM((NS, FF, NT), bf16), pltpu.SemaphoreType.DMA((NS,))]
     if post:
         part = pltpu.VMEM((NO, ROWS, NT), f32)
-        scratch += [pltpu.VMEM((TOK, 1536), bf16), pltpu.VMEM((ROWS, D), bf16), pltpu.VMEM((TOK, D), bf16),
+        scratch += attn_scratch() + [pltpu.VMEM((TOK, 1536), bf16), pltpu.VMEM((ROWS, D), bf16), pltpu.VMEM((TOK, D), bf16),
                     pltpu.VMEM((TOK, FF), bf16)] + [part] * 6 + [pltpu.SemaphoreType.DMA((NO,))] * 4
     if qkv:
         scratch += [pltpu.VMEM((TOK, D), bf16)]
@@ -566,7 +567,7 @@
         in_specs=specs,
         out_specs=tuple([vmem] * len(outs)),
         scratch_shapes=scratch,
-        compiler_params=pltpu.CompilerParams(vmem_limit_bytes=63 << 20, collective_id=2 + layer + (1 if post else 0),
+        compiler_params=pltpu.CompilerParams(vmem_limit_bytes=67043328, collective_id=2 + layer + (1 if post else 0),
                                              has_side_effects=True),
         cost_estimate=pl.CostEstimate(flops=TOK * moved, bytes_accessed=moved, transcendentals=0),
         name=f'dense{layer}{int(post)}{int(qkv)}',
@@ -602,11 +603,11 @@
         hidden = tokens
         q_send, kv_send = dense(0, False, True, hidden, **proj)
         for layer in range(layers):
-            o = attention(q_send.reshape(XN, GRP, TOK, HD), kv_send)
+            q_send = q_send.reshape(XN, GRP, TOK, HD)
             if layer + 1 < layers:
-                hidden, q_send, kv_send = dense(layer, True, True, hidden, o=o, **ffn, **proj)
+                hidden, q_send, kv_send = dense(layer, True, True, hidden, q_send=q_send, kv_send=kv_send, **ffn, **proj)
             else:
-                hidden, = dense(layer, True, False, hidden, o=o, **ffn)
+                hidden, = dense(layer, True, False, hidden, q_send=q_send, kv_send=kv_send, **ffn)
         return hidden
 
     return jax.shard_map(

time: 210 us -> 200 us (0.952)
  local copies, waits for them, and re-layouts: 7.73 us -> 2 us
  Pallas kernels: 200 us -> 196 us
    pallas_call x2 -> x0, Pallas kernels: 109 us -> none  [attention(): pl.pallas_call(attn_kernel, out_shape=jax.ShapeDtypeStruct((XN, 4, GRP, S...]
    pallas_call x3, Pallas kernels: 91 us -> 196 us  [dense(): pl.pallas_call(functools.partial(dense_kernel, layer, post, qkv), out_sha...]
    unnamed x13 -> x1, local copies, waits for them, and re-layouts: 7.64 us -> 1.92 us
where the time goes in v6:
time: 200 us
  Pallas kernels  196 us (98%)
  local copies, waits for them, and re-layouts  2 us (1%)
    pallas_call x3, Pallas kernels, dense(): pl.pallas_call(functools.partial(dense_kernel, layer, post, qkv), out_sha...  196 us

profile of v6, /device:TPU:1, one launch (start us, length us, event | category | flops | bytes accessed | tf_op | source)
XLA Modules:
  0.0 199.8 jit_solution(1295475114612058535)
XLA Ops:
  0.0 0.1 broadcast_subtract_fusion
  0.1 0.1 add_convert_fusion
  0.2 0.1 convert_element_type.11
  0.3 0.4 fusion
  0.7 0.8 pad_maximum_fusion
  1.5 9.8 %dense001.1 = (bf16[12,192,128]{2,1,0:T(8,128)(2,1)}, bf16[4,2,192,128]{3,2,1,0:T(8,128)(2,1)}) custom-call(bf16[96,3072]{1,0:T(8,128)(2,1)} %refs_0_.3, bf16[2,3072]{1,0:T(2,128)(2,1)} %refs_8_.1, f32[192,128]{1,0:T(8,128)} %get-tuple-element.20.refs_2_.refs_9_, f32[192,128]{1,0:T(8,128)} %get-tuple-element.21.refs_3_.refs_10_, ...), custom_call_target="tpu_custom_call" | custom-call | flops 3221225472 | bytes 16777216 | tf_op jit(solution)/shard_map/dense001/pallas_call | solution.py:564
  11.3 98.1 %dense011.1 = (bf16[96,3072]{1,0:T(8,128)(2,1)}, bf16[12,192,128]{2,1,0:T(8,128)(2,1)}, bf16[4,2,192,128]{3,2,1,0:T(8,128)(2,1)}) custom-call(bf16[96,3072]{1,0:T(8,128)(2,1)} %refs_0_.3, bf16[4,3,192,128]{3,2,1,0:T(8,128)(2,1)} %bitcast.10, bf16[4,2,192,128]{3,2,1,0:T(8,128)(2,1)} %get-tuple-element.11.refs_2_, bf16[2,3072]{1,0:T(2,128)(2,1)} %refs_3_.3, ...), custom_call_target="tpu_custom_call" | custom-call | flops 20333985792 | bytes 105906176 | tf_op jit(solution)/shard_map/dense011/pallas_call | solution.py:564
  109.5 88.4 %dense110.1 = bf16[96,3072]{1,0:T(8,128)(2,1)} custom-call(bf16[96,3072]{1,0:T(8,128)(2,1)} %get-tuple-element.12.refs_0_, bf16[4,3,192,128]{3,2,1,0:T(8,128)(2,1)} %bitcast.11, bf16[4,2,192,128]{3,2,1,0:T(8,128)(2,1)} %get-tuple-element.14.refs_2_, bf16[2,3072]{1,0:T(2,128)(2,1)} %refs_3_.3, bf16[2,1536,3072]{2,1,0:T(8,128)(2,1)} %bitcast.7, ...), custom_call_target="tpu_custom_call" | custom-call | flops 17112760320 | bytes 89128960 | tf_op jit(solution)/shard_map/dense110/pallas_call | solution.py:564
  197.8 1.9 copy.12
  (3 shorter events, 0.0 us)

commit v7 on v6

--- a/solution.py
+++ b/solution.py
@@ -424,6 +424,8 @@
         return pltpu.make_async_remote_copy(src_ref=src, dst_ref=dst, send_sem=ssem, recv_sem=rsem, device_id=sibling,
                                             device_id_type=pl.DeviceIdType.MESH)
 
+    pending = []
+
     def normed(src, gain_row, nrm, idx):
         ss = jnp.zeros((ROWS, 1), jnp.float32)
         for j in range(NO):
@@ -433,9 +435,12 @@
         for j in range(NO):
             sl = slice(j * NT, (j + 1) * NT)
             nrm[0:ROWS, sl] = (src[:, sl].astype(jnp.float32) * inv * gain_row[:, sl]).astype(jnp.bfloat16)
-        c = send(nrm.at[pl.ds(0, ROWS)], nrm.at[pl.ds(ROWS, ROWS)], sn.at[idx], rn.at[idx])
-        c.start()
-        return c
+            part = pl.ds(j * NT, NT)
+            c = send(nrm.at[pl.ds(0, ROWS), part], nrm.at[pl.ds(ROWS, ROWS), part], sn.at[idx, j], rn.at[idx, j])
+            c.start()
+            pending.append(c)
+        for c in pending[-NO:]:
+            c.wait_recv()
 
     def part_copy(snd, rcv, ss, rs, i):
         return send(snd.at[i], rcv.at[i], ss.at[i], rs.at[i])
@@ -446,7 +451,6 @@
             sl = slice(j * NT, (j + 1) * NT)
             out[:, sl] = (base[:, sl].astype(jnp.float32) + (acc[j] + rcv[j])).astype(jnp.bfloat16)
 
-    pending = []
     if post:
         for blk in range(4):
             row = pl.multiple_of(jnp.where(t_me == blk // 2, 0, ROWS) + (blk % 2) * SEG, 16)
@@ -467,9 +471,7 @@
 
         lax.fori_loop(0, NO // 2, o_step, 0)
         residual(hidden, acc1, rcv1, hmid, snd1, s1, r1)
-        c = normed(hmid, nm_mlp[...].astype(jnp.float32)[layer:layer + 1], nrm1, 0)
-        c.wait_recv()
-        pending.append(c)
+        normed(hmid, nm_mlp[...].astype(jnp.float32)[layer:layer + 1], nrm1, 0)
 
         def g_step(i, carry):
             t = g0 + 2 * i
@@ -501,9 +503,7 @@
         cur = hidden
     if qkv:
         nl = layer + 1 if post else layer
-        c = normed(cur, nm_attn[...].astype(jnp.float32)[nl:nl + 1], nrm2, 1)
-        c.wait_recv()
-        pending.append(c)
+        normed(cur, nm_attn[...].astype(jnp.float32)[nl:nl + 1], nrm2, 1)
         mine = pl.ds(pl.multiple_of(t_me * ROWS, 16), ROWS)
         theirs = pl.ds(pl.multiple_of((1 - t_me) * ROWS, 16), ROWS)
 
@@ -559,7 +559,7 @@
                     pltpu.VMEM((TOK, FF), bf16)] + [part] * 6 + [pltpu.SemaphoreType.DMA((NO,))] * 4
     if qkv:
         scratch += [pltpu.VMEM((TOK, D), bf16)]
-    scratch += [pltpu.SemaphoreType.DMA((2,))] * 2
+    scratch += [pltpu.SemaphoreType.DMA((2, NO))] * 2
     moved = (85 << 20 if post else 0) + (16 << 20 if qkv else 0)
     return pl.pallas_call(
         functools.partial(dense_kernel, layer, post, qkv),

time: 200 us -> 200 us (level)
  no operation moved by 1% of the time
where the time goes in v7:
time: 200 us
  Pallas kernels  197 us (98%)
  local copies, waits for them, and re-layouts  2 us (1%)
    pallas_call x3, Pallas kernels, dense(): pl.pallas_call(functools.partial(dense_kernel, layer, post, qkv), out_sha...  197 us

profile of v7, /device:TPU:1, one launch (start us, length us, event | category | flops | bytes accessed | tf_op | source)
XLA Modules:
  0.0 200.0 jit_solution(6644124395814617689)
XLA Ops:
  0.0 0.1 broadcast_subtract_fusion
  0.1 0.1 add_convert_fusion
  0.2 0.1 convert_element_type.11
  0.3 0.4 fusion
  0.7 0.8 pad_maximum_fusion
  1.5 9.9 %dense001.1 = (bf16[12,192,128]{2,1,0:T(8,128)(2,1)}, bf16[4,2,192,128]{3,2,1,0:T(8,128)(2,1)}) custom-call(bf16[96,3072]{1,0:T(8,128)(2,1)} %refs_0_.3, bf16[2,3072]{1,0:T(2,128)(2,1)} %refs_8_.1, f32[192,128]{1,0:T(8,128)} %get-tuple-element.20.refs_2_.refs_9_, f32[192,128]{1,0:T(8,128)} %get-tuple-element.21.refs_3_.refs_10_, ...), custom_call_target="tpu_custom_call" | custom-call | flops 3221225472 | bytes 16777216 | tf_op jit(solution)/shard_map/dense001/pallas_call | solution.py:564
  11.4 98.1 %dense011.1 = (bf16[96,3072]{1,0:T(8,128)(2,1)}, bf16[12,192,128]{2,1,0:T(8,128)(2,1)}, bf16[4,2,192,128]{3,2,1,0:T(8,128)(2,1)}) custom-call(bf16[96,3072]{1,0:T(8,128)(2,1)} %refs_0_.3, bf16[4,3,192,128]{3,2,1,0:T(8,128)(2,1)} %bitcast.10, bf16[4,2,192,128]{3,2,1,0:T(8,128)(2,1)} %get-tuple-element.11.refs_2_, bf16[2,3072]{1,0:T(2,128)(2,1)} %refs_3_.3, ...), custom_call_target="tpu_custom_call" | custom-call | flops 20333985792 | bytes 105906176 | tf_op jit(solution)/shard_map/dense011/pallas_call | solution.py:564
  109.5 88.5 %dense110.1 = bf16[96,3072]{1,0:T(8,128)(2,1)} custom-call(bf16[96,3072]{1,0:T(8,128)(2,1)} %get-tuple-element.12.refs_0_, bf16[4,3,192,128]{3,2,1,0:T(8,128)(2,1)} %bitcast.11, bf16[4,2,192,128]{3,2,1,0:T(8,128)(2,1)} %get-tuple-element.14.refs_2_, bf16[2,3072]{1,0:T(2,128)(2,1)} %refs_3_.3, bf16[2,1536,3072]{2,1,0:T(8,128)(2,1)} %bitcast.7, ...), custom_call_target="tpu_custom_call" | custom-call | flops 17112760320 | bytes 89128960 | tf_op jit(solution)/shard_map/dense110/pallas_call | solution.py:564
  198.0 1.9 copy.12
  (3 shorter events, 0.0 us)
